TPU v7x, 32 devices: a whole 2x2x4 slice. The times are simulated.
32 devices in a mesh: row: 8 (over z, core), col: 4 (over y, x).
Axes of the slice: x: 2, y: 2, z: 4, core: 2. Of those that a mesh axis runs over, the one named last changes fastest.
Arguments:
- schur_blocks: bfloat16 [4, 8, 8, 4, 256, 256], P(None, 'row', None, 'col'), may hold values from -0.1875 to 0.1875
- known_blocks: float32 [4, 8, 8, 4, 256, 256], P(None, 'row', None, 'col'), may hold values from -6 to 6
- eigen_pairs: float32 [4, 8, 2, 256, 256], P(None, 'row'), as said below
- eigenvalues: float32 [32, 256], replicated, may hold values from 1 to 8.95, as said below
Outputs:
- updated: float32 [4, 8, 8, 4, 256, 256], P(None, 'row', None, 'col')
Inputs may be any that keep to these rules, and one draw needn't show every extreme that they name: For each block, eigen_pairs[a, r, 0] is unit upper triangular and eigen_pairs[a, r, 1] is its inverse. `eigenvalues`: row i lies within 1 + i / 4 and 1.2 + i / 4.
All inputs are finite; a program needn't handle non-finite values.
Results may differ from a plain program's by a relative error of at most 0.0017.
Values may be sent and summed in bfloat16 or wider, within the bound.
No kernel may reach another device: no remote copies, remote signals or barrier semaphores. Data moves between devices by JAX's collectives and lax.ppermute only.
A program may use at most 192 MiB of HBM per device.

v0:
```python
import jax
import jax.numpy as jnp
from jax import lax
from jax.experimental import pallas as pl
from jax.experimental.pallas import tpu as pltpu
from jax.sharding import PartitionSpec as P


FIRST = 8
DIAGS = 4
VMEM_BYTES = 67_043_328


def shifted(block, axis, distance):
    devices = range(lax.axis_size(axis))
    route = [((i - distance) % len(devices), i) for i in devices]
    return lax.ppermute(block, axis, route)


def pick_rows(stacked, indices):
    return jax.vmap(lambda source, chosen: source[chosen])(stacked, indices)


def full_dot(left_side, right_side):
    return jnp.einsum(
        "apq,aqr->apr",
        left_side,
        right_side,
        precision=lax.Precision.HIGHEST,
        preferred_element_type=jnp.float32,
    )


def right_terms(known_rows, schur_rows, known_cols, schur_cols, offsets, usable, distance):
    band_width = known_rows.shape[1]
    reach_back = distance[:, :, None] - offsets
    first_mask = usable & (offsets >= 1) & (reach_back >= 0) & (reach_back <= FIRST - 1)
    second_mask = usable & (offsets <= FIRST - 1) & (reach_back >= 1)
    clipped = jnp.clip(reach_back, 0, band_width - 1)
    known_pick = jnp.where(first_mask[..., None, None], pick_rows(known_rows, clipped), 0)
    schur_pick = jnp.where(second_mask[..., None, None], -pick_rows(schur_rows, clipped), 0)
    left_side = jnp.concatenate([known_pick, schur_pick], axis=2)
    right_side = jnp.concatenate([schur_cols, known_cols], axis=2)
    return jnp.einsum(
        "atepq,ateqr->atpr", left_side, right_side, preferred_element_type=jnp.float32
    )


def body(schur_blocks, known_blocks, eigen_pairs, eigenvalues):
    row_count = lax.axis_size("row")
    col_count = lax.axis_size("col")
    row_index = lax.axis_index("row")
    col_index = lax.axis_index("col")
    schur_local = schur_blocks[:, 0, :, 0]
    known_local = known_blocks[:, 0, :, 0]
    pairs_local = eigen_pairs[:, 0]
    block_rows = schur_local.shape[0]
    block_cols = schur_local.shape[1]
    blocks_total = block_rows * row_count
    band_width = FIRST + DIAGS
    row_slots = -(-band_width // col_count)
    col_slots = -(-band_width // row_count)
    per_row = -(-DIAGS // col_count)
    row_ids = jnp.arange(block_rows, dtype=jnp.int32) * row_count + row_index
    col_ids = jnp.arange(block_cols, dtype=jnp.int32) * col_count + col_index
    band_range = jnp.arange(band_width, dtype=jnp.int32)
    row_range = jnp.arange(block_rows, dtype=jnp.int32)
    row_offsets = (
        jnp.mod(col_index - row_ids, col_count)[:, None]
        + jnp.arange(row_slots, dtype=jnp.int32)[None, :] * col_count
    )
    row_reach = row_ids[:, None] + row_offsets
    row_valid = (row_offsets < band_width) & (row_reach < blocks_total)
    row_pick = jnp.clip(row_reach // col_count, 0, block_cols - 1)
    known_send = jnp.where(
        row_valid[..., None, None], pick_rows(known_local, row_pick), 0.0
    ).astype(jnp.bfloat16)
    schur_send = jnp.where(row_valid[..., None, None], pick_rows(schur_local, row_pick), 0)
    known_recv, schur_recv = (
        lax.all_gather(known_send[None], "col", axis=0, tiled=True),
        lax.all_gather(schur_send[None], "col", axis=0, tiled=True),
    )
    row_source = jnp.mod(row_ids[:, None] + band_range[None, :], col_count)
    row_slot = (band_range // col_count)[None, :]
    known_rows = known_recv[row_source, row_range[:, None], row_slot]
    schur_rows = schur_recv[row_source, row_range[:, None], row_slot]
    col_offsets = (
        jnp.mod(col_ids - row_index, row_count)[:, None]
        + jnp.arange(col_slots, dtype=jnp.int32)[None, :] * row_count
    )
    col_reach = col_ids[:, None] - col_offsets
    col_valid = (col_offsets < band_width) & (col_reach >= 0)
    col_pick = jnp.clip(col_reach // row_count, 0, block_rows - 1)
    known_down = jnp.where(
        col_valid[..., None, None], pick_rows(jnp.swapaxes(known_local, 0, 1), col_pick), 0.0
    ).astype(jnp.bfloat16)
    schur_down = jnp.where(
        col_valid[..., None, None], pick_rows(jnp.swapaxes(schur_local, 0, 1), col_pick), 0
    )
    target_first = -((col_index - row_ids - FIRST) // col_count)
    target_block = target_first[:, None] + jnp.arange(per_row, dtype=jnp.int32)[None, :]
    target_cols = target_block * col_count + col_index
    distance = target_cols - row_ids[:, None]
    active = (target_block < block_cols) & (distance <= FIRST + DIAGS - 1)
    target_clip = jnp.clip(target_block, 0, block_cols - 1)
    own_strip = jnp.stack([known_down, schur_down])
    collected = jnp.zeros((row_count,) + own_strip.shape, jnp.bfloat16)
    collected = collected.at[row_index].set(own_strip)
    reach_rows = min(row_count, band_width)
    carried = own_strip
    for step in range(1, reach_rows):
        carried = shifted(carried, "row", row_count - 1)
        collected = collected.at[jnp.mod(row_index + step, row_count)].set(carried)
    known_all = collected[:, 0]
    schur_all = collected[:, 1]
    col_source = jnp.mod(target_cols[:, :, None] - band_range[None, None, :], row_count)
    col_slot = (band_range // row_count)[None, None, :]
    known_cols = known_all[col_source, target_clip[:, :, None], col_slot]
    schur_cols = schur_all[col_source, target_clip[:, :, None], col_slot]
    offsets = jnp.broadcast_to(band_range[None, None, :], col_source.shape)
    totals = right_terms(
        known_rows,
        schur_rows,
        known_cols,
        schur_cols,
        offsets,
        jnp.ones(offsets.shape, jnp.bool_),
        distance,
    )
    kept_cols = schur_cols[:, :, :DIAGS]
    pair_list = []
    for distance_now in range(FIRST, FIRST + DIAGS):
        lag = distance_now % row_count
        receiver = jnp.mod(row_index - lag, row_count)
        wanted = jnp.clip(
            (row_range * row_count + receiver + distance_now) // row_count, 0, block_rows - 1
        )
        sending = pairs_local[wanted]
        if lag == 0:
            pair_list.append(sending)
        else:
            pair_list.append(
                shifted(sending.astype(jnp.bfloat16), "row", row_count - lag).astype(sending.dtype)
            )
    vec_left = pairs_local[:, 0]
    inv_left = pairs_local[:, 1]
    lam_left = eigenvalues[row_ids]
    output = known_local
    for distance_now in range(FIRST, FIRST + DIAGS):
        hitting = active & (distance == distance_now)
        solving = jnp.any(hitting, axis=1)
        chosen = jnp.sum(jnp.where(hitting[..., None, None], totals, 0.0), axis=1)
        block_col = jnp.sum(jnp.where(hitting, target_clip, 0), axis=1)
        block_ids = jnp.clip(block_col * col_count + col_index, 0, blocks_total - 1)
        vec_right = pair_list[distance_now - FIRST][:, 0]
        inv_right = pair_list[distance_now - FIRST][:, 1]
        lam_right = eigenvalues[block_ids]
        spacing = lam_left[:, :, None] - lam_right[:, None, :]
        spacing = jnp.where(solving[:, None, None], spacing, 1.0)
        mixed_block = full_dot(full_dot(inv_left, chosen), vec_right) / spacing
        solved = full_dot(full_dot(vec_left, mixed_block), inv_right)
        solved = jnp.where(solving[:, None, None], solved, 0.0)
        placing = solving[:, None] & (
            jnp.arange(block_cols, dtype=jnp.int32)[None, :] == block_col[:, None]
        )
        output = jnp.where(placing[:, :, None, None], solved[:, None], output)
        if distance_now < FIRST + DIAGS - 1:
            rounded = solved.astype(jnp.bfloat16)
            for gap in range(1, FIRST + DIAGS - distance_now):
                row_new = shifted(rounded, "col", gap)
                receiver = jnp.mod(row_index - gap, row_count)
                wanted = jnp.clip(
                    (row_range * row_count + receiver + gap) // row_count, 0, block_rows - 1
                )
                col_new = shifted(rounded[wanted], "row", row_count - gap)
                growing = active & (distance - distance_now == gap)
                known_from_row = row_new[:, None]
                known_from_col = col_new[:, None]
                schur_from_row = schur_rows[:, gap][:, None]
                schur_from_col = kept_cols[:, :, gap]
                left_side = jnp.stack(
                    [
                        jnp.where(growing[..., None, None], known_from_row, 0),
                        jnp.where(growing[..., None, None], -schur_from_row, 0),
                    ],
                    axis=2,
                )
                right_side = jnp.stack([schur_from_col, known_from_col], axis=2)
                totals = totals + jnp.einsum(
                    "atepq,ateqr->atpr", left_side, right_side, preferred_element_type=jnp.float32
                )
    return output[:, None, :, None]


ROUNDS = {0: [[(0, 1)]], 1: [[(1, 2), (0, 3)], [(0, 2), (1, 3)]], 2: [[(2, 3)]]}


def lag_of(r, c, cols):
    return lax.rem(c - r + 2 * cols * FIRST, cols)


def lead_of(r, c, cols):
    return lax.div(r - c + lag_of(r, c, cols), cols)


def any_spec():
    return pl.BlockSpec(memory_space=pltpu.HBM)


def place_spec():
    return pl.BlockSpec(memory_space=pltpu.SMEM)


def mod_add(value, shift, size):
    return lax.rem(value + shift + 4 * size, size)


def mirrored(step, c, cols):
    return jnp.where(c >= cols // 2, -step, step)


def column_picks(place, step, chips, aim_core, rows, cols, a):
    r, c = place[0], place[1]
    chip = mod_add(lax.div(r, 2), -step, chips)
    lead = lead_of(2 * chip + aim_core, c, cols)
    j = rows * a + FIRST + cols * lead + c
    off_f = lax.rem(j - r + rows, rows)
    off_s = 1 + lax.rem(j - r - 1 + rows, rows)
    return lax.div(j - off_f - r, rows), lax.div(j - off_s - r, rows), (j - c) // cols


def pack(known, schur, place, aim_core, rows, cols, first):
    block_rows, block_cols, bs = known.shape[0], known.shape[1], known.shape[2]
    count = block_rows - 1
    chips = rows // 2
    slots = FIRST // cols

    n_rows = slots if first else 0
    shapes = [(count, 2, bs, bs)] * (n_rows + chips) + ([(count, bs, bs)] if first else [])
    total = count * (n_rows + chips)

    def kernel(place, known_ref, schur_ref, *refs):
        outs, refs = refs[: len(shapes)], refs[len(shapes) :]
        bufs, refs = refs[: len(shapes)], refs[len(shapes) :]
        wide, in_sems, out_sems, far_sems = refs
        r, c = place[0], place[1]
        lead = lead_of(r, c, cols)
        groups = []
        for step in [chips // 2] + [x for x in range(1, chips) if x != chips // 2] + [0]:
            picks = []
            for a in range(count):
                way = step if first else mirrored(step, c, cols)
                f_row, s_row, b = column_picks(place, way, chips, aim_core, rows, cols, a)
                picks.append(((f_row, b), (s_row, b)))
            groups.append((n_rows + step, picks))
        extra = jnp.where(lag_of(r, c, cols) == 0, 1, 0)
        for slot in range(n_rows):
            picks = []
            for a in range(count):
                base = (rows // cols) * a + lead + slot
                picks.append(((a, base), (a, base + extra)))
            groups.insert(1 + slot, (slot, picks))

        def clip(at):
            return jnp.clip(at[0], 0, block_rows - 1), jnp.clip(at[1], 0, block_cols - 1)

        n = 0
        plans = []
        for at, picks in groups:
            mine = []
            for a, (f_at, s_at) in enumerate(picks):
                f_at, s_at = clip(f_at), clip(s_at)
                low = pltpu.make_async_copy(known_ref.at[f_at[0], f_at[1]], wide.at[n], in_sems.at[n, 0])
                thin = pltpu.make_async_copy(
                    schur_ref.at[s_at[0], s_at[1]], bufs[at].at[a, 1], in_sems.at[n, 1]
                )
                low.start()
                thin.start()
                mine.append((n, low, thin, a))
                n += 1
            plans.append((at, mine))
        fars = []
        if first:
            for a in range(count):
                at = clip((a, (rows // cols) * a + FIRST // cols + lead))
                far = pltpu.make_async_copy(schur_ref.at[at[0], at[1]], bufs[-1].at[a], far_sems.at[a])
                far.start()
                fars.append(far)
        sends = []
        for at, mine in plans:
            for n, low, thin, a in mine:
                low.wait()
                bufs[at][a, 0] = wide[n].astype(jnp.bfloat16)
                thin.wait()
            out = pltpu.make_async_copy(bufs[at], outs[at], out_sems.at[at])
            out.start()
            sends.append(out)
        if first:
            for far in fars:
                far.wait()
            out = pltpu.make_async_copy(bufs[-1], outs[-1], out_sems.at[len(shapes) - 1])
            out.start()
            sends.append(out)
        for out in sends:
            out.wait()

    return pl.pallas_call(
        kernel,
        in_specs=[place_spec(), any_spec(), any_spec()],
        out_specs=[any_spec()] * len(shapes),
        out_shape=[jax.ShapeDtypeStruct(x, jnp.bfloat16) for x in shapes],
        scratch_shapes=[pltpu.VMEM(x, jnp.bfloat16) for x in shapes]
        + [
            pltpu.VMEM((total, bs, bs), jnp.float32),
            pltpu.SemaphoreType.DMA((total, 2)),
            pltpu.SemaphoreType.DMA((len(shapes),)),
            pltpu.SemaphoreType.DMA((count,)),
        ],
        compiler_params=pltpu.CompilerParams(vmem_limit_bytes=VMEM_BYTES),
        cost_estimate=pl.CostEstimate(
            flops=total * bs * bs * 200, bytes_accessed=total * bs * bs * 10, transcendentals=0
        ),
        name="pack_first" if first else "pack_late",
    )(place, known, schur)


def copy_blocks(known):
    block_rows, block_cols, bs = known.shape[0], known.shape[1], known.shape[2]

    def kernel(source, out):
        out[...] = source[...]

    spec = pl.BlockSpec((1, block_cols, bs, bs), lambda n: (n, 0, 0, 0))
    return pl.pallas_call(
        kernel,
        grid=(block_rows,),
        in_specs=[spec],
        out_specs=spec,
        out_shape=jax.ShapeDtypeStruct(known.shape, known.dtype),
        compiler_params=pltpu.CompilerParams(vmem_limit_bytes=VMEM_BYTES),
        cost_estimate=pl.CostEstimate(
            flops=known.size * 1000, bytes_accessed=known.size * 8, transcendentals=0
        ),
        name="copy_known",
    )(known)


def mm(left, right):
    return jnp.dot(left, right, preferred_element_type=jnp.float32)


def own_lag(place, cols):
    r, c = place[0], place[1]
    lag = lag_of(r, c, cols)
    return r, c, lag, (lax.rem(r, 2) == 1) & (lag == cols - 1)


def offsets_of(r, lag, step, crossed, rows):
    chip = mod_add(lax.div(r, 2), step, rows // 2)
    core = lax.rem(r, 2)
    origin = 2 * chip + (1 - core if crossed else core)
    aim = r + lag
    return lax.rem(aim - origin + rows, rows), 1 + lax.rem(aim - origin - 1 + 2 * rows, rows)


def sum_base(place, row_parts, columns, after, own_far, row_far, col_far, late, rows, cols):
    count, _, bs, _ = row_parts[0][0].shape
    slots = len(row_parts[0])
    reach = FIRST + DIAGS - 1
    far_in = [own_far] + row_far + col_far
    flat_rows = [x for parts in row_parts for x in parts]
    n_rows, n_cols, n_far, n_after = len(flat_rows), len(columns), len(far_in), len(after)

    def kernel(place, *refs):
        row_in, refs = refs[:n_rows], refs[n_rows:]
        col_in, refs = refs[:n_cols], refs[n_cols:]
        far_ref, refs = refs[:n_far], refs[n_far:]
        outs, refs = refs[: 3 + (1 if n_after else 0)], refs[3 + (1 if n_after else 0) :]
        total_out, keep_row, keep_col = outs[:3]
        row_f, row_s, col_buf, col_far_buf, left_buf, total, sems = refs
        r, c, lag, is_late = own_lag(place, cols)
        active = is_late if late else jnp.logical_not(is_late)

        @pl.when(active)
        def _():
            sem = 0

            def plan(src, dst):
                nonlocal sem
                copy = pltpu.make_async_copy(src, dst, sems.at[sem])
                sem += 1
                return copy

            def begin(src, dst):
                copy = plan(src, dst)
                copy.start()
                return copy

            copies = []
            for n, ref in enumerate(row_in):
                shift = lag_of(r, jnp.bitwise_xor(c, n // slots), cols)
                shift_s = lax.rem(shift + cols - 1, cols)
                slot = n % slots
                copies.append(begin(ref.at[:, 0], row_f.at[:, cols * slot + shift]))
                copies.append(begin(ref.at[:, 1], row_s.at[:, cols * slot + shift_s]))
            far_rows = []
            for g in range(1 + len(row_far)):
                copy = plan(far_ref[g], row_s.at[:, jnp.maximum(FIRST + lag - g - 1, FIRST)])
                pl.when(lag > g)(copy.start)
                far_rows.append((g, copy))
            for g in range(1 + len(col_far)):
                src = far_ref[0] if g == 0 else far_ref[len(row_far) + g]
                copies.append(begin(src, col_far_buf.at[g]))
            col_copies = [begin(ref, col_buf.at[n]) for n, ref in enumerate(col_in)]
            for copy in copies:
                copy.wait()
            for g, copy in far_rows:
                pl.when(lag > g)(copy.wait)
            keeps = [(None, begin(row_s.at[:, pl.ds(0, DIAGS - 1)], keep_row))]

            def lefts(step, crossed, a):
                way = mirrored(step, c, cols) if late else step
                off_f, off_s = offsets_of(r, lag, way, crossed, rows)
                at_f = FIRST + lag - off_s
                left = row_f[a, jnp.minimum(at_f, FIRST - 1)]
                left = jnp.where(at_f < FIRST, left, jnp.zeros_like(left))
                return left, row_s[a, FIRST + lag - off_f - 1]

            for n, (step, crossed) in enumerate(after):
                for a in range(count):
                    left_buf[a, 2 * n], left_buf[a, 2 * n + 1] = lefts(step, crossed, a)
            if n_after:
                keeps.append((None, begin(left_buf, outs[3])))
            for a in range(count):
                part = jnp.zeros((bs, bs), jnp.float32)
                for g in range(1 + len(col_far)):
                    at = jnp.where(r + g >= rows, jnp.minimum(a + 1, count - 1), a)
                    left = row_f[a, g]
                    left = jnp.where(lag > g, left, jnp.zeros_like(left))
                    part = part + mm(left, col_far_buf[g, at])
                total[a] = part
            for n, (_, step, crossed) in enumerate(columns):
                way = mirrored(step, c, cols) if late else step
                off_s = offsets_of(r, lag, way, crossed, rows)[1]
                col_copies[n].wait()
                for a in range(count):
                    with_s, with_f = lefts(step, crossed, a)
                    total[a] += mm(with_s, col_buf[n, a, 1]) - mm(with_f, col_buf[n, a, 0])
                save = plan(col_buf.at[n, :, 1], keep_col.at[:, jnp.minimum(off_s, DIAGS - 1) - 1])
                pl.when(off_s < DIAGS)(save.start)
                keeps.append((off_s, save))
            out = begin(total, total_out)
            for off_s, copy in keeps:
                if off_s is None:
                    copy.wait()
                else:
                    pl.when(off_s < DIAGS)(copy.wait)
            out.wait()

    out_shape = [
        jax.ShapeDtypeStruct((count, bs, bs), jnp.float32),
        jax.ShapeDtypeStruct((count, DIAGS - 1, bs, bs), jnp.bfloat16),
        jax.ShapeDtypeStruct((count, DIAGS - 1, bs, bs), jnp.bfloat16),
    ]
    if n_after:
        out_shape.append(jax.ShapeDtypeStruct((count, 2 * n_after, bs, bs), jnp.bfloat16))
    return pl.pallas_call(
        kernel,
        in_specs=[place_spec()] + [any_spec()] * (n_rows + n_cols + n_far),
        out_specs=[any_spec()] * len(out_shape),
        out_shape=out_shape,
        scratch_shapes=[
            pltpu.VMEM((count, FIRST, bs, bs), jnp.bfloat16),
            pltpu.VMEM((count, reach, bs, bs), jnp.bfloat16),
            pltpu.VMEM((n_cols, count, 2, bs, bs), jnp.bfloat16),
            pltpu.VMEM((1 + len(col_far), count, bs, bs), jnp.bfloat16),
            pltpu.VMEM((count, max(2 * n_after, 1), bs, bs), jnp.bfloat16),
            pltpu.VMEM((count, bs, bs), jnp.float32),
            pltpu.SemaphoreType.DMA((2 * n_rows + n_far + 2 * n_cols + 4,)),
        ],
        compiler_params=pltpu.CompilerParams(vmem_limit_bytes=VMEM_BYTES),
        cost_estimate=pl.CostEstimate(
            flops=count * 18 * 2 * bs**3, bytes_accessed=count * 40 * bs * bs * 2, transcendentals=0
        ),
        name="sum_late" if late else "sum_early",
    )(place, *flat_rows, *[x for x, _, _ in columns], *far_in)


def sum_rest(place, columns, sums, late, rows, cols):
    total_in, keep_row, keep_col, lefts = sums
    count, bs = total_in.shape[0], total_in.shape[1]
    n_cols = len(columns)

    def kernel(place, *refs):
        col_in, refs = refs[:n_cols], refs[n_cols:]
        old, _, left_in, total_out, keep_out, col_buf, left_buf, total, sems = refs
        r, c, lag, is_late = own_lag(place, cols)

        @pl.when(is_late if late else jnp.logical_not(is_late))
        def _():
            copies = [pltpu.make_async_copy(old, total, sems.at[0])]
            copies.append(pltpu.make_async_copy(left_in, left_buf, sems.at[1]))
            for n, ref in enumerate(col_in):
                copies.append(pltpu.make_async_copy(ref, col_buf.at[n], sems.at[2 + n]))
            for copy in copies:
                copy.start()
            for copy in copies:
                copy.wait()
            saves = []
            for n, (_, step, crossed) in enumerate(columns):
                way = mirrored(step, c, cols) if late else step
                off_s = offsets_of(r, lag, way, crossed, rows)[1]
                save = pltpu.make_async_copy(
                    col_buf.at[n, :, 1],
                    keep_out.at[:, jnp.minimum(off_s, DIAGS - 1) - 1],
                    sems.at[2 + n],
                )
                pl.when(off_s < DIAGS)(save.start)
                saves.append((off_s, save))
            for a in range(count):
                part = total[a]
                for n in range(n_cols):
                    part = part + mm(left_buf[a, 2 * n], col_buf[n, a, 1])
                    part = part - mm(left_buf[a, 2 * n + 1], col_buf[n, a, 0])
                total[a] = part
            out = pltpu.make_async_copy(total, total_out, sems.at[0])
            out.start()
            for off_s, save in saves:
                pl.when(off_s < DIAGS)(save.wait)
            out.wait()

    first = 1 + n_cols
    total, keep_col = pl.pallas_call(
        kernel,
        in_specs=[place_spec()] + [any_spec()] * (n_cols + 3),
        out_specs=[any_spec()] * 2,
        out_shape=[
            jax.ShapeDtypeStruct(total_in.shape, total_in.dtype),
            jax.ShapeDtypeStruct(keep_col.shape, keep_col.dtype),
        ],
        input_output_aliases={first: 0, first + 1: 1},
        scratch_shapes=[
            pltpu.VMEM((n_cols, count, 2, bs, bs), jnp.bfloat16),
            pltpu.VMEM(lefts.shape, jnp.bfloat16),
            pltpu.VMEM((count, bs, bs), jnp.float32),
            pltpu.SemaphoreType.DMA((2 + n_cols,)),
        ],
        compiler_params=pltpu.CompilerParams(vmem_limit_bytes=VMEM_BYTES),
        cost_estimate=pl.CostEstimate(
            flops=count * 4 * 2 * bs**3, bytes_accessed=count * 12 * bs * bs * 2, transcendentals=0
        ),
        name="rest_late" if late else "sum_rest",
    )(place, *[x for x, _, _ in columns], total_in, keep_col, lefts)
    return total, keep_row, keep_col


def halves(value):
    high = value.astype(jnp.bfloat16)
    return high, (value - high.astype(jnp.float32)).astype(jnp.bfloat16)


def solve_stage(
    stage, place, output, carried, sums, late_sums, row_new, col_new, far_pairs, own_pairs, spacing, rows, cols
):
    count, bs = sums[0].shape[0], sums[0].shape[1]
    block_cols = output.shape[1]
    last = stage == DIAGS - 1
    two = last and late_sums is not None
    groups = [list(sums)] + ([list(late_sums)] if two else [])
    flat = [x for group in groups for x in group]
    n_new = len(row_new)

    passed = [] if carried is None else [carried]

    def kernel(place, out_in, *refs):
        refs = refs[len(passed) :]
        group_refs, refs = refs[: len(flat)], refs[len(flat) :]
        row_in, refs = refs[:n_new], refs[n_new:]
        col_in, refs = refs[:n_new], refs[n_new:]
        pair_far, pair_own, space_in, out, sent, refs = *refs[:5], refs[5:]
        total, keep_r, keep_c, row_buf, col_buf, far_buf, own_buf, space, solved, narrow, sems = refs
        r, c = place[0], place[1]
        lag = lag_of(r, c, cols)
        is_late = (lax.rem(r, 2) == 1) & (lag == cols - 1)

        @pl.when(lag == stage)
        def _():
            sem = 0

            def plan(src, dst):
                nonlocal sem
                copy = pltpu.make_async_copy(src, dst, sems.at[sem])
                sem += 1
                return copy

            small = []
            for n in range(n_new):
                small.append(plan(row_in[n], row_buf.at[n]))
                small.append(plan(col_in[n], col_buf.at[n]))
            ours = plan(pair_own.at[pl.ds(0, count)], own_buf)
            small += [plan(pair_far, far_buf), plan(space_in, space)]
            targets = [total] + ([keep_r, keep_c] if n_new else [])
            first_sem = sem
            for at, group in enumerate([group_refs[:3], group_refs[3:]][: len(groups)]):
                chosen = is_late if at == 1 else jnp.logical_not(is_late)
                for i, dst in enumerate(targets):
                    copy = pltpu.make_async_copy(group[i], dst, sems.at[first_sem + i])
                    if two:
                        pl.when(chosen)(copy.start)
                    else:
                        copy.start()
            for copy in small + [ours]:
                copy.start()
            for i, dst in enumerate(targets):
                pltpu.make_async_copy(group_refs[i], dst, sems.at[first_sem + i]).wait()
            for copy in small + [ours]:
                copy.wait()
            lead = lead_of(r, c, cols)
            wrapped = jnp.where(r + lag >= rows, 1, 0)
            each = range(count)
            right = [total[a] for a in each]
            for n in range(n_new):
                g = stage - n
                for a in each:
                    at = jnp.where(r + g >= rows, jnp.minimum(a + 1, count - 1), a)
                    right[a] = right[a] + mm(row_buf[n, a], keep_c[a, g - 1])
                    right[a] = right[a] - mm(keep_r[a, g - 1], col_buf[n, at])
            far = [jnp.minimum(a + wrapped, count - 1) for a in each]

            def from_left(side, values):
                left = [halves(own_buf[a, side]) for a in each]
                value = [halves(x) for x in values]
                return [
                    mm(left[a][0], value[a][0])
                    + (mm(left[a][0], value[a][1]) + mm(left[a][1], value[a][0]))
                    for a in each
                ]

            def from_right(values, side):
                value = [halves(x) for x in values]
                return [
                    mm(value[a][0], far_buf[far[a], side]) + mm(value[a][1], far_buf[far[a], side])
                    for a in each
                ]

            mixed = from_right(from_left(1, right), 0)
            mixed = [mixed[a] / space[a] for a in each]
            answer = from_right(from_left(0, mixed), 1)
            for a in each:
                narrow[a] = answer[a].astype(jnp.bfloat16)
                solved[a] = answer[a]
            copies = []
            send = None
            if not last:
                send = pltpu.make_async_copy(narrow, sent, sems.at[sem])
                send.start()
            for a in range(count):
                at = (rows // cols) * a + FIRST // cols + lead
                copy = pltpu.make_async_copy(
                    solved.at[a], out.at[a, jnp.minimum(at, block_cols - 1)], sems.at[a]
                )
                pl.when(at < block_cols)(copy.start)
                copies.append((at, copy))
            for at, copy in copies:
                pl.when(at < block_cols)(copy.wait)
            if send is not None:
                send.wait()

    n_in = 2 + len(passed) + len(flat) + 2 * n_new + 3
    half = max(n_new, 1)
    return pl.pallas_call(
        kernel,
        in_specs=[place_spec()] + [any_spec()] * (n_in - 1),
        out_specs=[any_spec()] * 2,
        out_shape=[
            jax.ShapeDtypeStruct(output.shape, output.dtype),
            jax.ShapeDtypeStruct((count, bs, bs), jnp.bfloat16),
        ],
        input_output_aliases={1 + i: i for i in range(1 + len(passed))},
        scratch_shapes=[
            pltpu.VMEM((count, bs, bs), jnp.float32),
            pltpu.VMEM((count, DIAGS - 1, bs, bs), jnp.bfloat16),
            pltpu.VMEM((count, DIAGS - 1, bs, bs), jnp.bfloat16),
            pltpu.VMEM((half, count, bs, bs), jnp.bfloat16),
            pltpu.VMEM((half, count, bs, bs), jnp.bfloat16),
            pltpu.VMEM((count, 2, bs, bs), jnp.bfloat16),
            pltpu.VMEM((count, 2, bs, bs), jnp.float32),
            pltpu.VMEM((count, bs, bs), jnp.float32),
            pltpu.VMEM((count, bs, bs), jnp.float32),
            pltpu.VMEM((count, bs, bs), jnp.bfloat16),
            pltpu.SemaphoreType.DMA((2 * n_new + 6 + count,)),
        ],
        compiler_params=pltpu.CompilerParams(vmem_limit_bytes=VMEM_BYTES),
        cost_estimate=pl.CostEstimate(
            flops=count * 12 * 2 * bs**3, bytes_accessed=count * 20 * bs * bs * 2, transcendentals=0
        ),
    )(place, output, *passed, *flat, *row_new, *col_new, far_pairs, own_pairs, spacing)


def banded_body(schur_blocks, known_blocks, eigen_pairs, eigenvalues):
    return banded_steps(schur_blocks, known_blocks, eigen_pairs, eigenvalues)


def banded_steps(schur_blocks, known_blocks, eigen_pairs, eigenvalues):
    rows = lax.axis_size("row")
    cols = lax.axis_size("col")
    r = lax.axis_index("row")
    c = lax.axis_index("col")
    schur = schur_blocks[:, 0, :, 0]
    known = known_blocks[:, 0, :, 0]
    pairs = eigen_pairs[:, 0]
    count = known.shape[0] - 1
    chips = rows // 2
    slots = FIRST // cols
    devices = [(i, k) for i in range(rows) for k in range(cols)]

    def lag(i, k):
        return (k - i) % cols

    def send(block, move, keep=lambda i, k: True, senders=None):
        routes = []
        for i, k in devices:
            if senders is not None and lag(i, k) not in senders:
                continue
            to = move(i, k)
            to = (to[0] % rows, to[1] % cols)
            if keep(*to):
                routes.append((i * cols + k, to[0] * cols + to[1]))
        return lax.ppermute(block, ("row", "col"), routes)

    def late_core(i, k):
        return lag(i, k) == cols - 1 and i % 2 == 1

    place = jnp.stack([r, c]).astype(jnp.int32)
    packed = pack(known, schur, place, 0, rows, cols, True)
    own_parts, col_packs, own_far = packed[:slots], packed[slots:-1], packed[-1]
    early = {0: col_packs[0]}
    for step in range(1, chips):
        early[step] = send(col_packs[step], lambda i, j, s=step: (i - 2 * s, j))
    row_parts = [list(own_parts)]
    for k in (1, 2):
        row_parts.append([send(part, lambda i, j, k=k: (i, j ^ k)) for part in own_parts])
    row_parts.append(
        [
            send(row_parts[1][0], lambda i, j: (i, j ^ 2)),
            send(row_parts[2][1], lambda i, j: (i, j ^ 1)),
        ]
    )
    row_far, col_far = [], []
    for g in range(1, DIAGS - 1):
        takes = lambda i, k, g=g: lag(i, k) > g
        row_far.append(send(own_far, lambda i, j, g=g: (i, j + g), takes))
        col_far.append(send(own_far, lambda i, j, g=g: (i - g, j), takes))
    pair_list = [lax.optimization_barrier((pairs, own_far))[0][1:].astype(jnp.bfloat16)]
    for g in range(1, DIAGS):
        takes = lambda i, k, g=g: lag(i, k) == g
        pair_list.append(send(pair_list[-1], lambda i, j: (i - 1, j), takes))
    lag_here = lag_of(r, c, cols)
    own_ids = jnp.arange(count, dtype=jnp.int32) * rows + r
    far_ids = jnp.minimum(own_ids + FIRST + lag_here, eigenvalues.shape[0] - 1)
    spacing = eigenvalues[own_ids][:, :, None] - eigenvalues[far_ids][:, None, :]
    spacing = lax.optimization_barrier((spacing, own_far))[0]
    late_packs = pack(known, schur, place, 1, rows, cols, False)
    output = copy_blocks(known)

    crossed = {n: send(early[n], lambda i, j: (i ^ 1, j)) for n in range(chips)}
    late = [(late_packs[0], 0, False)]
    late_last = []
    for step in range(chips):

        def onward(i, j, step=step):
            return i - 2 * (step if j < cols // 2 else -step), j

        def onward_across(i, j, onward=onward):
            return onward(i, j)[0] ^ 1, j

        into = late_last if step == chips // 2 else late
        if step:
            into.append((send(late_packs[step], onward, late_core), step, False))
        into.append((send(late_packs[step], onward_across, late_core), step, True))
    final = chips // 2
    last = [(early[final], final, False), (crossed[final], final, True)]
    ready = []
    for step in range(chips):
        if step != final:
            ready += [(early[step], step, False), (crossed[step], step, True)]
    sums = sum_base(
        place, row_parts, ready, [x[1:] for x in last], own_far, row_far, col_far, False, rows, cols
    )
    sums = sum_rest(place, last, sums, False, rows, cols)
    late_sums = sum_base(
        place, row_parts, late, [x[1:] for x in late_last], own_far, row_far, col_far, True, rows, cols
    )
    late_sums = sum_rest(place, late_last, late_sums, True, rows, cols)
    carried = None
    row_new = {}
    col_new = {}
    for stage in range(DIAGS):
        output, carried = solve_stage(
            stage,
            place,
            output,
            carried,
            sums,
            late_sums,
            [row_new[n, stage] for n in range(stage)],
            [col_new[n, stage] for n in range(stage)],
            pair_list[stage],
            pairs,
            spacing,
            rows,
            cols,
        )
        for hops in ROUNDS.get(stage, ()):
            by_lag = dict(hops)
            takes = set(by_lag.values())

            def gap(i, k):
                return by_lag.get(lag(i, k), lag(i, k)) - lag(i, k)

            def wanted(i, k):
                return lag(i, k) in takes

            across = send(carried, lambda i, j: (i, j + gap(i, j)), wanted, by_lag)
            upward = send(carried, lambda i, j: (i - gap(i, j), j), wanted, by_lag)
            for hop in hops:
                row_new[hop] = across
                col_new[hop] = upward
    return output[:, None, :, None]


def solution(mesh):
    rows, cols = mesh.shape["row"], mesh.shape["col"]
    banded = rows == FIRST and cols == DIAGS
    return jax.shard_map(
        banded_body if banded else body,
        mesh=mesh,
        in_specs=(
            P(None, "row", None, "col", None, None),
            P(None, "row", None, "col", None, None),
            P(None, "row", None, None, None),
            P(),
        ),
        out_specs=P(None, "row", None, "col", None, None),
        check_vma=False,
    )
```

profile of v0, /device:TPU:17, one launch (start us, length us, event | category | flops | bytes accessed | tf_op | source)
XLA Modules:
  0.0 232.1 jit_solution(10215309881388415823)
XLA Ops:
  0.6 6.6 %pack_first.1 = (bf16[3,2,256,256]{3,2,1,0:T(8,128)(2,1)}, bf16[3,2,256,256]{3,2,1,0:T(8,128)(2,1)}, bf16[3,2,256,256]{3,2,1,0:T(8,128)(2,1)}, bf16[3,2,256,256]...) custom-call(s32[2]{0:T(128)} %pad_add_fusion.place, ...), custom_call_target="tpu_custom_call" | custom-call | flops 235929600 | bytes 11796480 | tf_op jit(solution)/shard_map/pack_first/pallas_call | solution.py:307
  7.2 1.3 collective-permute-start.13
  8.5 1.3 collective-permute-start.14
  9.8 3.3 %collective-permute-start.5 = (bf16[3,2,256,256]{3,2,1,0:T(8,128)(2,1)}, bf16[3,2,256,256]{3,2,1,0:T(8,128)(2,1)}, u32[]{:S(2)}, u32[]{:S(2)}) collective-permute-start(bf16[3,2,256,256]{3,2,1,0:T(8,128)(2,1)} %get-tuple-element.39.refs_1_), channel_id=1, source_target_pairs={{0,2},{1,3},{2,0},{3,1},{4,6},{5,7},{6,4},{7,5},{8,10},{9,11},{10,... | collective-permute-start | bytes 2359304 | tf_op jit(solution)/shard_map/ppermute | solution.py:729
  13.1 1.4 collective-permute-start.3
  14.5 3.0 %collective-permute-done.13.refs_15_ = bf16[3,256,256]{2,1,0:T(8,128)(2,1)S(1)} collective-permute-done((bf16[3,256,256]{2,1,0:T(8,128)(2,1)}, bf16[3,256,256]{2,1,0:T(8,128)(2,1)S(1)}, u32[]{:S(2)}, u32[]{:S(2)}) %collective-permute-start.13) | collective-permute-done | bytes 393248 | tf_op jit(solution)/shard_map/ppermute | solution.py:729
  17.5 1.3 collective-permute-start.15
  18.8 6.2 %collective-permute-done.14.refs_16_ = bf16[3,256,256]{2,1,0:T(8,128)(2,1)S(1)} collective-permute-done((bf16[3,256,256]{2,1,0:T(8,128)(2,1)}, bf16[3,256,256]{2,1,0:T(8,128)(2,1)S(1)}, u32[]{:S(2)}, u32[]{:S(2)}) %collective-permute-start.14) | collective-permute-done | bytes 393248 | tf_op jit(solution)/shard_map/ppermute | solution.py:729
  25.0 1.3 collective-permute-start.16
  26.3 7.7 %collective-permute-done.15.refs_17_ = bf16[3,256,256]{2,1,0:T(8,128)(2,1)S(1)} collective-permute-done((bf16[3,256,256]{2,1,0:T(8,128)(2,1)}, bf16[3,256,256]{2,1,0:T(8,128)(2,1)S(1)}, u32[]{:S(2)}, u32[]{:S(2)}) %collective-permute-start.15) | collective-permute-done | bytes 393248 | tf_op jit(solution)/shard_map/ppermute | solution.py:729
  34.0 2.0 collective-permute-done.16.refs_18_
  36.1 1.5 collective-permute-start.11
  37.5 3.5 %collective-permute-done.5.refs_5_ = bf16[3,2,256,256]{3,2,1,0:T(8,128)(2,1)} collective-permute-done((bf16[3,2,256,256]{3,2,1,0:T(8,128)(2,1)}, bf16[3,2,256,256]{3,2,1,0:T(8,128)(2,1)}, u32[]{:S(2)}, u32[]{:S(2)}) %collective-permute-start.5) | collective-permute-done | bytes 786464 | tf_op jit(solution)/shard_map/ppermute | solution.py:729
  41.0 4.1 %collective-permute-done.3.refs_3_ = bf16[3,2,256,256]{3,2,1,0:T(8,128)(2,1)S(1)} collective-permute-done((bf16[3,2,256,256]{3,2,1,0:T(8,128)(2,1)}, bf16[3,2,256,256]{3,2,1,0:T(8,128)(2,1)S(1)}, u32[]{:S(2)}, u32[]{:S(2)}) %collective-permute-start.3) | collective-permute-done | bytes 786464 | tf_op jit(solution)/shard_map/ppermute | solution.py:729
  45.1 10.0 %collective-permute-done.4.refs_4_ = bf16[3,2,256,256]{3,2,1,0:T(8,128)(2,1)S(1)} collective-permute-done((bf16[3,2,256,256]{3,2,1,0:T(8,128)(2,1)}, bf16[3,2,256,256]{3,2,1,0:T(8,128)(2,1)S(1)}, u32[]{:S(2)}, u32[]{:S(2)}) %collective-permute-start.4) | collective-permute-done | bytes 786464 | tf_op jit(solution)/shard_map/ppermute | solution.py:729
  56.0 16.5 %collective-permute-done.11.refs_12_ = bf16[3,2,256,256]{3,2,1,0:T(8,128)(2,1)} collective-permute-done((bf16[3,2,256,256]{3,2,1,0:T(8,128)(2,1)}, bf16[3,2,256,256]{3,2,1,0:T(8,128)(2,1)}, u32[]{:S(2)}, u32[]{:S(2)}) %collective-permute-start.11) | collective-permute-done | bytes 786464 | tf_op jit(solution)/shard_map/ppermute | solution.py:729
  72.5 16.3 %collective-permute-start.10 = (bf16[3,2,256,256]{3,2,1,0:T(8,128)(2,1)}, bf16[3,2,256,256]{3,2,1,0:T(8,128)(2,1)}, u32[]{:S(2)}, u32[]{:S(2)}) collective-permute-start(bf16[3,2,256,256]{3,2,1,0:T(8,128)(2,1)} %collective-permute-done.9.refs_10_), channel_id=1, source_target_pairs={{0,4},{1,5},{2,6},{3,7},{4,0},{5,1},{6,2},{7,3},{8,12},{9,13},{10,... | collective-permute-start | bytes 2359304 | tf_op jit(solution)/shard_map/ppermute | solution.py:729
  88.9 13.5 %collective-permute-done.refs_0_ = bf16[3,2,256,256]{3,2,1,0:T(8,128)(2,1)} collective-permute-done((bf16[3,2,256,256]{3,2,1,0:T(8,128)(2,1)}, bf16[3,2,256,256]{3,2,1,0:T(8,128)(2,1)}, u32[]{:S(2)}, u32[]{:S(2)}) %collective-permute-start) | collective-permute-done | bytes 786464 | tf_op jit(solution)/shard_map/ppermute | solution.py:729
  102.9 1.3 gather_fusion
  104.2 1.3 gather_fusion.1
  105.5 2.4 %slice.11.refs_3_ = bf16[3,2,256,256]{3,2,1,0:T(8,128)(2,1)} slice(f32[4,2,256,256]{3,2,1,0:T(8,128)} %bitcast.15), slice={[1:4], [0:2], [0:256], [0:256]} | slice | bytes 1572864 | tf_op jit(solution)/shard_map/slice | solution.py:754
  109.8 1.6 collective-permute-start.19
  111.3 7.1 %copy_known.1.out_in = f32[4,8,256,256]{3,2,1,0:T(8,128)} custom-call(f32[4,8,256,256]{3,2,1,0:T(8,128)} %bitcast.13), custom_call_target="tpu_custom_call" | custom-call | flops 2097152000 | bytes 16777216 | tf_op jit(solution)/shard_map/copy_known/pallas_call | solution.py:334
  121.0 1.4 collective-permute-start.17
  122.4 1.4 collective-permute-start.18
  123.9 5.0 %pack_late.1 = (bf16[3,2,256,256]{3,2,1,0:T(8,128)(2,1)}, bf16[3,2,256,256]{3,2,1,0:T(8,128)(2,1)}, bf16[3,2,256,256]{3,2,1,0:T(8,128)(2,1)}, bf16[3,2,256,256]{3,2,1,0:T(8,128)(2,1)}) custom-call(s32[2]{0:T(128)} %pad_add_fusion.place, f32[4,8,256,256]{3,2,1,0:T(8,128)} %bitcast.14, bf16[4,8,256,256]{3,2,1,0:T(8,128)(2,1)} %bitcast.21), custom_call_target="tpu_custom_call" | custom-call | flops 157286400 | bytes 7864320 | tf_op jit(solution)/shard_map/pack_late/pallas_call | solution.py:307
  128.9 1.3 collective-permute-start.27
  130.2 1.3 collective-permute-start.28
  131.5 1.3 collective-permute-start.29
  132.8 1.6 collective-permute-start.24
  135.1 1.3 collective-permute-start.20
  136.4 15.7 %collective-permute-done.27.refs_9_ = bf16[3,2,256,256]{3,2,1,0:T(8,128)(2,1)} collective-permute-done((bf16[3,2,256,256]{3,2,1,0:T(8,128)(2,1)}, bf16[3,2,256,256]{3,2,1,0:T(8,128)(2,1)}, u32[]{:S(2)}, u32[]{:S(2)}) %collective-permute-start.27) | collective-permute-done | bytes 786464 | tf_op jit(solution)/shard_map/ppermute | solution.py:729
  152.2 1.3 collective-permute-start.21
  153.5 9.0 %collective-permute-done.28.refs_10_ = bf16[3,2,256,256]{3,2,1,0:T(8,128)(2,1)} collective-permute-done((bf16[3,2,256,256]{3,2,1,0:T(8,128)(2,1)}, bf16[3,2,256,256]{3,2,1,0:T(8,128)(2,1)}, u32[]{:S(2)}, u32[]{:S(2)}) %collective-permute-start.28) | collective-permute-done | bytes 786464 | tf_op jit(solution)/shard_map/ppermute | solution.py:729
  162.4 1.3 collective-permute-start.22
  164.9 1.3 collective-permute-start.30
  166.2 1.3 collective-permute-start.23
  167.5 1.3 collective-permute-start.31
  168.8 1.9 collective-permute-start.25
  171.3 1.3 collective-permute-start.26
  172.6 6.2 %collective-permute-done.23.refs_7_.refs_10_ = bf16[3,256,256]{2,1,0:T(8,128)(2,1)} collective-permute-done((bf16[3,256,256]{2,1,0:T(8,128)(2,1)}, bf16[3,256,256]{2,1,0:T(8,128)(2,1)}, u32[]{:S(2)}, u32[]{:S(2)}) %collective-permute-start.23) | collective-permute-done | bytes 393248 | tf_op jit(solution)/shard_map/ppermute | solution.py:729
  178.8 1.3 collective-permute-start.34
  181.1 27.3 %collective-permute-done.30.refs_12_ = bf16[3,2,256,256]{3,2,1,0:T(8,128)(2,1)} collective-permute-done((bf16[3,2,256,256]{3,2,1,0:T(8,128)(2,1)}, bf16[3,2,256,256]{3,2,1,0:T(8,128)(2,1)}, u32[]{:S(2)}, u32[]{:S(2)}) %collective-permute-start.30) | collective-permute-done | bytes 786464 | tf_op jit(solution)/shard_map/ppermute | solution.py:729
  208.3 1.3 collective-permute-start.32
  209.6 1.3 collective-permute-start.33
  210.9 9.6 %sum_late.1 = (f32[3,256,256]{2,1,0:T(8,128)}, bf16[3,3,256,256]{3,2,1,0:T(8,128)(2,1)}, bf16[3,3,256,256]{3,2,1,0:T(8,128)(2,1)}, bf16[3,4,256,256]{3,2,1,0:T(8,128)(2,1)}) custom-call(s32[2]{0:T(128)} %pad_add_fusion.place, bf16[3,2,256,256]{3,2,1,0:T(8,128)(2,1)} %get-tuple-element.38.refs_0_, bf16[3,2,256,256]{3,2,1,0:T(8,128)(2,1)} %get-tuple-element.39.refs_1_, ...), custom_call_target="tpu_custom_call" | custom-call | flops 1811939328 | bytes 15728640 | tf_op jit(solution)/shard_map/sum_late/pallas_call | solution.py:467
  220.5 4.3 %rest_late.1 = (f32[3,256,256]{2,1,0:T(8,128)}, bf16[3,3,256,256]{3,2,1,0:T(8,128)(2,1)}) custom-call(s32[2]{0:T(128)} %pad_add_fusion.place, bf16[3,2,256,256]{3,2,1,0:T(8,128)(2,1)} %collective-permute-done.25.refs_0_, bf16[3,2,256,256]{3,2,1,0:T(8,128)(2,1)} %collective-permute-done.26.refs_1_, ...), custom_call_target="tpu_custom_call", output_to_operand_aliasing={{0}: (3, {}), {1}: (4, {})} | custom-call | flops 402653184 | bytes 4718592 | tf_op jit(solution)/shard_map/rest_late/pallas_call | solution.py:533
  224.8 7.1 %shard_map.49 = (f32[4,8,256,256]{3,2,1,0:T(8,128)}, bf16[3,256,256]{2,1,0:T(8,128)(2,1)}) custom-call(s32[2]{0:T(128)} %pad_add_fusion.place, f32[4,8,256,256]{3,2,1,0:T(8,128)} %get-tuple-element.56.out_in, bf16[3,256,256]{2,1,0:T(8,128)(2,1)} %get-tuple-element.57.refs_0_, ...), custom_call_target="tpu_custom_call", output_to_operand_aliasing={{0}: (1, {}), {1}: (2, {})} | custom-call | flops 1207959552 | bytes 7864320 | tf_op jit(solution)/shard_map/pallas_call | solution.py:671
  (57 shorter events, 10.0 us)
Async XLA Ops:
  7.2 10.4 %collective-permute-start.13 = (bf16[3,256,256]{2,1,0:T(8,128)(2,1)}, bf16[3,256,256]{2,1,0:T(8,128)(2,1)S(1)}, u32[]{:S(2)}, u32[]{:S(2)}) collective-permute-start(bf16[3,256,256]{2,1,0:T(8,128)(2,1)} %get-tuple-element.43.refs_14_), channel_id=1, source_target_pairs={{1,2},{2,3},{6,7},{7,4},{8,9},{11,8},{12,13},{13,14},{17,18},{18,1... | collective-permute-start | bytes 1179656 | tf_op jit(solution)/shard_map/ppermute | solution.py:729
  8.5 16.5 %collective-permute-start.14 = (bf16[3,256,256]{2,1,0:T(8,128)(2,1)}, bf16[3,256,256]{2,1,0:T(8,128)(2,1)S(1)}, u32[]{:S(2)}, u32[]{:S(2)}) collective-permute-start(bf16[3,256,256]{2,1,0:T(8,128)(2,1)} %get-tuple-element.43.refs_14_), channel_id=1, source_target_pairs={{1,3},{6,4},{11,9},{12,14},{17,19},{22,20},{27,25},{28,30}} | collective-permute-start | bytes 1179656 | tf_op jit(solution)/shard_map/ppermute | solution.py:729
  9.8 26.3 %collective-permute-start.2 = (bf16[3,2,256,256]{3,2,1,0:T(8,128)(2,1)}, bf16[3,2,256,256]{3,2,1,0:T(8,128)(2,1)S(1)}, u32[]{:S(2)}, u32[]{:S(2)}) collective-permute-start(bf16[3,2,256,256]{3,2,1,0:T(8,128)(2,1)} %get-tuple-element.38.refs_0_), channel_id=1, source_target_pairs={{0,1},{1,0},{2,3},{3,2},{4,5},{5,4},{6,7},{7,6},{8,9},{9,8},{10,11... | collective-permute-start | bytes 2359304 | tf_op jit(solution)/shard_map/ppermute | solution.py:729
  9.8 31.2 %collective-permute-start.5 = (bf16[3,2,256,256]{3,2,1,0:T(8,128)(2,1)}, bf16[3,2,256,256]{3,2,1,0:T(8,128)(2,1)}, u32[]{:S(2)}, u32[]{:S(2)}) collective-permute-start(bf16[3,2,256,256]{3,2,1,0:T(8,128)(2,1)} %get-tuple-element.39.refs_1_), channel_id=1, source_target_pairs={{0,2},{1,3},{2,0},{3,1},{4,6},{5,7},{6,4},{7,5},{8,10},{9,11},{10,... | collective-permute-start | bytes 2359304 | tf_op jit(solution)/shard_map/ppermute | solution.py:729
  13.1 32.0 %collective-permute-start.3 = (bf16[3,2,256,256]{3,2,1,0:T(8,128)(2,1)}, bf16[3,2,256,256]{3,2,1,0:T(8,128)(2,1)S(1)}, u32[]{:S(2)}, u32[]{:S(2)}) collective-permute-start(bf16[3,2,256,256]{3,2,1,0:T(8,128)(2,1)} %get-tuple-element.39.refs_1_), channel_id=1, source_target_pairs={{0,1},{1,0},{2,3},{3,2},{4,5},{5,4},{6,7},{7,6},{8,9},{9,8},{10,11... | collective-permute-start | bytes 2359304 | tf_op jit(solution)/shard_map/ppermute | solution.py:729
  17.5 8.7 %copy-start.4 = (bf16[3,256,256]{2,1,0:T(8,128)(2,1)}, bf16[3,256,256]{2,1,0:T(8,128)(2,1)S(1)}, u32[]{:S(2)}) copy-start(bf16[3,256,256]{2,1,0:T(8,128)(2,1)S(1)} %collective-permute-done.13.refs_15_) | copy-start | bytes 1179652
  17.5 16.5 %collective-permute-start.15 = (bf16[3,256,256]{2,1,0:T(8,128)(2,1)}, bf16[3,256,256]{2,1,0:T(8,128)(2,1)S(1)}, u32[]{:S(2)}, u32[]{:S(2)}) collective-permute-start(bf16[3,256,256]{2,1,0:T(8,128)(2,1)} %get-tuple-element.43.refs_14_), channel_id=1, source_target_pairs={{1,29},{2,30},{6,2},{7,3},{8,4},{11,7},{12,8},{13,9},{17,13},{18,1... | collective-permute-start | bytes 1179656 | tf_op jit(solution)/shard_map/ppermute | solution.py:729
  25.0 1.3 copy-start.5
  25.0 11.1 %collective-permute-start.16 = (bf16[3,256,256]{2,1,0:T(8,128)(2,1)}, bf16[3,256,256]{2,1,0:T(8,128)(2,1)S(1)}, u32[]{:S(2)}, u32[]{:S(2)}) collective-permute-start(bf16[3,256,256]{2,1,0:T(8,128)(2,1)} %get-tuple-element.43.refs_14_), channel_id=1, source_target_pairs={{1,25},{6,30},{11,3},{12,4},{17,9},{22,14},{27,19},{28,20}} | collective-permute-start | bytes 1179656 | tf_op jit(solution)/shard_map/ppermute | solution.py:729
  34.0 22.0 %copy-start.6 = (bf16[3,256,256]{2,1,0:T(8,128)(2,1)}, bf16[3,256,256]{2,1,0:T(8,128)(2,1)S(1)}, u32[]{:S(2)}) copy-start(bf16[3,256,256]{2,1,0:T(8,128)(2,1)S(1)} %collective-permute-done.15.refs_17_) | copy-start | bytes 1179652
  34.0 21.1 %collective-permute-start.4 = (bf16[3,2,256,256]{3,2,1,0:T(8,128)(2,1)}, bf16[3,2,256,256]{3,2,1,0:T(8,128)(2,1)S(1)}, u32[]{:S(2)}, u32[]{:S(2)}) collective-permute-start(bf16[3,2,256,256]{3,2,1,0:T(8,128)(2,1)} %get-tuple-element.38.refs_0_), channel_id=1, source_target_pairs={{0,2},{1,3},{2,0},{3,1},{4,6},{5,7},{6,4},{7,5},{8,10},{9,11},{10,... | collective-permute-start | bytes 2359304 | tf_op jit(solution)/shard_map/ppermute | solution.py:729
  36.1 36.5 %copy-start.7 = (bf16[3,256,256]{2,1,0:T(8,128)(2,1)}, bf16[3,256,256]{2,1,0:T(8,128)(2,1)S(1)}, u32[]{:S(2)}) copy-start(bf16[3,256,256]{2,1,0:T(8,128)(2,1)S(1)} %collective-permute-done.16.refs_18_) | copy-start | bytes 1179652
  36.1 19.9 %collective-permute-start.9 = (bf16[3,2,256,256]{3,2,1,0:T(8,128)(2,1)}, bf16[3,2,256,256]{3,2,1,0:T(8,128)(2,1)}, u32[]{:S(2)}, u32[]{:S(2)}) collective-permute-start(bf16[3,2,256,256]{3,2,1,0:T(8,128)(2,1)} %get-tuple-element.41), channel_id=1, source_target_pairs={{0,24},{1,25},{2,26},{3,27},{4,28},{5,29},{6,30},{7,31},{8,0},{9,1... | collective-permute-start | bytes 2359304 | tf_op jit(solution)/shard_map/ppermute | solution.py:729
  36.1 19.0 %copy-start = (bf16[3,2,256,256]{3,2,1,0:T(8,128)(2,1)}, bf16[3,2,256,256]{3,2,1,0:T(8,128)(2,1)S(1)}, u32[]{:S(2)}) copy-start(bf16[3,2,256,256]{3,2,1,0:T(8,128)(2,1)S(1)} %collective-permute-done.2.refs_2_) | copy-start | bytes 2359300
  36.1 36.5 %collective-permute-start.11 = (bf16[3,2,256,256]{3,2,1,0:T(8,128)(2,1)}, bf16[3,2,256,256]{3,2,1,0:T(8,128)(2,1)}, u32[]{:S(2)}, u32[]{:S(2)}) collective-permute-start(bf16[3,2,256,256]{3,2,1,0:T(8,128)(2,1)} %get-tuple-element.42), channel_id=1, source_target_pairs={{0,8},{1,9},{2,10},{3,11},{4,12},{5,13},{6,14},{7,15},{8,16},{9,17... | collective-permute-start | bytes 2359304 | tf_op jit(solution)/shard_map/ppermute | solution.py:729
  41.0 47.8 %collective-permute-start.8 = (bf16[3,2,256,256]{3,2,1,0:T(8,128)(2,1)}, bf16[3,2,256,256]{3,2,1,0:T(8,128)(2,1)}, u32[]{:S(2)}, u32[]{:S(2)}) collective-permute-start(bf16[3,2,256,256]{3,2,1,0:T(8,128)(2,1)} %get-tuple-element.40.refs_8_), channel_id=1, source_target_pairs={{0,4},{1,5},{2,6},{3,7},{4,0},{5,1},{6,2},{7,3},{8,12},{9,13},{10,... | collective-permute-start | bytes 2359304 | tf_op jit(solution)/shard_map/ppermute | solution.py:729
  45.1 10.0 %copy-start.1 = (bf16[3,2,256,256]{3,2,1,0:T(8,128)(2,1)}, bf16[3,2,256,256]{3,2,1,0:T(8,128)(2,1)S(1)}, u32[]{:S(2)}) copy-start(bf16[3,2,256,256]{3,2,1,0:T(8,128)(2,1)S(1)} %collective-permute-done.3.refs_3_) | copy-start | bytes 2359300
  45.1 57.3 %collective-permute-start = (bf16[3,2,256,256]{3,2,1,0:T(8,128)(2,1)}, bf16[3,2,256,256]{3,2,1,0:T(8,128)(2,1)}, u32[]{:S(2)}, u32[]{:S(2)}) collective-permute-start(bf16[3,2,256,256]{3,2,1,0:T(8,128)(2,1)} %get-tuple-element.37), channel_id=1, source_target_pairs={{0,16},{1,17},{2,18},{3,19},{4,20},{5,21},{6,22},{7,23},{8,24},{9,... | collective-permute-start | bytes 2359304 | tf_op jit(solution)/shard_map/ppermute | solution.py:729
  55.1 0.9 copy-start.2
  55.1 53.8 %collective-permute-start.6 = (bf16[3,2,256,256]{3,2,1,0:T(8,128)(2,1)S(1)}, bf16[3,2,256,256]{3,2,1,0:T(8,128)(2,1)S(1)}, u32[]{:S(2)}, u32[]{:S(2)}) collective-permute-start(bf16[3,2,256,256]{3,2,1,0:T(8,128)(2,1)S(1)} %collective-permute-done.2.refs_2_), channel_id=1, source_target_pairs={{0,2},{1,3},{2,0},{3,1},{4,6},{5,7},{6,4},{7,5},{8,10},{9,11},{10,... | collective-permute-start | bytes 2359304 | tf_op jit(solution)/shard_map/ppermute | solution.py:729
  56.0 62.4 %collective-permute-start.7 = (bf16[3,2,256,256]{3,2,1,0:T(8,128)(2,1)}, bf16[3,2,256,256]{3,2,1,0:T(8,128)(2,1)}, u32[]{:S(2)}, u32[]{:S(2)}) collective-permute-start(bf16[3,2,256,256]{3,2,1,0:T(8,128)(2,1)} %collective-permute-done.5.refs_5_), channel_id=1, source_target_pairs={{0,1},{1,0},{2,3},{3,2},{4,5},{5,4},{6,7},{7,6},{8,9},{9,8},{10,11... | collective-permute-start | bytes 2359304 | tf_op jit(solution)/shard_map/ppermute | solution.py:729
  72.5 45.9 %collective-permute-start.10 = (bf16[3,2,256,256]{3,2,1,0:T(8,128)(2,1)}, bf16[3,2,256,256]{3,2,1,0:T(8,128)(2,1)}, u32[]{:S(2)}, u32[]{:S(2)}) collective-permute-start(bf16[3,2,256,256]{3,2,1,0:T(8,128)(2,1)} %collective-permute-done.9.refs_10_), channel_id=1, source_target_pairs={{0,4},{1,5},{2,6},{3,7},{4,0},{5,1},{6,2},{7,3},{8,12},{9,13},{10,... | collective-permute-start | bytes 2359304 | tf_op jit(solution)/shard_map/ppermute | solution.py:729
  88.8 29.6 %collective-permute-start.12 = (bf16[3,2,256,256]{3,2,1,0:T(8,128)(2,1)}, bf16[3,2,256,256]{3,2,1,0:T(8,128)(2,1)}, u32[]{:S(2)}, u32[]{:S(2)}) collective-permute-start(bf16[3,2,256,256]{3,2,1,0:T(8,128)(2,1)} %collective-permute-done.11.refs_12_), channel_id=1, source_target_pairs={{0,4},{1,5},{2,6},{3,7},{4,0},{5,1},{6,2},{7,3},{8,12},{9,13},{10,... | collective-permute-start | bytes 2359304 | tf_op jit(solution)/shard_map/ppermute | solution.py:729
  102.4 17.1 %collective-permute-start.1 = (bf16[3,2,256,256]{3,2,1,0:T(8,128)(2,1)}, bf16[3,2,256,256]{3,2,1,0:T(8,128)(2,1)}, u32[]{:S(2)}, u32[]{:S(2)}) collective-permute-start(bf16[3,2,256,256]{3,2,1,0:T(8,128)(2,1)} %collective-permute-done.refs_0_), channel_id=1, source_target_pairs={{0,4},{1,5},{2,6},{3,7},{4,0},{5,1},{6,2},{7,3},{8,12},{9,13},{10,... | collective-permute-start | bytes 2359304 | tf_op jit(solution)/shard_map/ppermute | solution.py:729
  108.9 0.9 copy-start.3
  109.8 21.7 %collective-permute-start.19 = (bf16[3,2,256,256]{3,2,1,0:T(8,128)(2,1)}, bf16[3,2,256,256]{3,2,1,0:T(8,128)(2,1)}, u32[]{:S(2)}, u32[]{:S(2)}) collective-permute-start(bf16[3,2,256,256]{3,2,1,0:T(8,128)(2,1)} %slice.11.refs_3_), channel_id=1, source_target_pairs={{0,28},{5,1},{10,6},{15,11},{16,12},{21,17},{26,22},{31,27}} | collective-permute-start | bytes 2359304 | tf_op jit(solution)/shard_map/ppermute | solution.py:729
  121.0 11.8 %collective-permute-start.17 = (bf16[3,256,256]{2,1,0:T(8,128)(2,1)}, bf16[3,256,256]{2,1,0:T(8,128)(2,1)}, u32[]{:S(2)}, u32[]{:S(2)}) collective-permute-start(bf16[3,256,256]{2,1,0:T(8,128)(2,1)} %get-tuple-element.53.refs_0_), channel_id=1, source_target_pairs={{0,1},{5,6},{10,11},{15,12},{16,17},{21,22},{26,27},{31,28}} | collective-permute-start | bytes 1179656 | tf_op jit(solution)/shard_map/ppermute | solution.py:729
  122.4 11.9 %collective-permute-start.18 = (bf16[3,256,256]{2,1,0:T(8,128)(2,1)}, bf16[3,256,256]{2,1,0:T(8,128)(2,1)}, u32[]{:S(2)}, u32[]{:S(2)}) collective-permute-start(bf16[3,256,256]{2,1,0:T(8,128)(2,1)} %get-tuple-element.53.refs_0_), channel_id=1, source_target_pairs={{0,28},{5,1},{10,6},{15,11},{16,12},{21,17},{26,22},{31,27}} | collective-permute-start | bytes 1179656 | tf_op jit(solution)/shard_map/ppermute | solution.py:729
  128.9 23.3 %collective-permute-start.27 = (bf16[3,2,256,256]{3,2,1,0:T(8,128)(2,1)}, bf16[3,2,256,256]{3,2,1,0:T(8,128)(2,1)}, u32[]{:S(2)}, u32[]{:S(2)}) collective-permute-start(bf16[3,2,256,256]{3,2,1,0:T(8,128)(2,1)} %get-tuple-element.59.refs_8_), channel_id=1, source_target_pairs={{0,4},{10,14},{16,20},{26,30}} | collective-permute-start | bytes 2359304 | tf_op jit(solution)/shard_map/ppermute | solution.py:729
  130.2 32.3 %collective-permute-start.28 = (bf16[3,2,256,256]{3,2,1,0:T(8,128)(2,1)}, bf16[3,2,256,256]{3,2,1,0:T(8,128)(2,1)}, u32[]{:S(2)}, u32[]{:S(2)}) collective-permute-start(bf16[3,2,256,256]{3,2,1,0:T(8,128)(2,1)} %get-tuple-element.60), channel_id=1, source_target_pairs={{6,14},{12,4},{22,30},{28,20}} | collective-permute-start | bytes 2359304 | tf_op jit(solution)/shard_map/ppermute | solution.py:729
  131.5 33.4 %collective-permute-start.29 = (bf16[3,2,256,256]{3,2,1,0:T(8,128)(2,1)}, bf16[3,2,256,256]{3,2,1,0:T(8,128)(2,1)}, u32[]{:S(2)}, u32[]{:S(2)}) collective-permute-start(bf16[3,2,256,256]{3,2,1,0:T(8,128)(2,1)} %get-tuple-element.60), channel_id=1, source_target_pairs={{2,14},{8,4},{18,30},{24,20}} | collective-permute-start | bytes 2359304 | tf_op jit(solution)/shard_map/ppermute | solution.py:729
  132.8 33.4 %collective-permute-start.24 = (bf16[3,2,256,256]{3,2,1,0:T(8,128)(2,1)}, bf16[3,2,256,256]{3,2,1,0:T(8,128)(2,1)}, u32[]{:S(2)}, u32[]{:S(2)}) collective-permute-start(bf16[3,2,256,256]{3,2,1,0:T(8,128)(2,1)} %collective-permute-done.19.refs_6_), channel_id=1, source_target_pairs={{1,29},{6,2},{11,7},{12,8},{17,13},{22,18},{27,23},{28,24}} | collective-permute-start | bytes 2359304 | tf_op jit(solution)/shard_map/ppermute | solution.py:729
  135.1 32.3 %collective-permute-start.20 = (bf16[3,256,256]{2,1,0:T(8,128)(2,1)}, bf16[3,256,256]{2,1,0:T(8,128)(2,1)}, u32[]{:S(2)}, u32[]{:S(2)}) collective-permute-start(bf16[3,256,256]{2,1,0:T(8,128)(2,1)} %get-tuple-element.55.refs_0_), channel_id=1, source_target_pairs={{0,2},{1,3},{5,7},{6,4},{10,8},{11,9},{12,14},{15,13},{16,18},{17,... | collective-permute-start | bytes 1179656 | tf_op jit(solution)/shard_map/ppermute | solution.py:729
  152.2 16.6 %collective-permute-start.21 = (bf16[3,256,256]{2,1,0:T(8,128)(2,1)}, bf16[3,256,256]{2,1,0:T(8,128)(2,1)}, u32[]{:S(2)}, u32[]{:S(2)}) collective-permute-start(bf16[3,256,256]{2,1,0:T(8,128)(2,1)} %get-tuple-element.55.refs_0_), channel_id=1, source_target_pairs={{0,3},{1,2},{5,4},{6,7},{10,9},{11,8},{12,13},{15,14},{16,19},{17,... | collective-permute-start | bytes 1179656 | tf_op jit(solution)/shard_map/ppermute | solution.py:729
  162.4 8.8 %collective-permute-start.22 = (bf16[3,256,256]{2,1,0:T(8,128)(2,1)}, bf16[3,256,256]{2,1,0:T(8,128)(2,1)}, u32[]{:S(2)}, u32[]{:S(2)}) collective-permute-start(bf16[3,256,256]{2,1,0:T(8,128)(2,1)} %get-tuple-element.55.refs_0_), channel_id=1, source_target_pairs={{0,24},{1,25},{5,29},{6,30},{10,2},{11,3},{12,4},{15,7},{16,8},{17... | collective-permute-start | bytes 1179656 | tf_op jit(solution)/shard_map/ppermute | solution.py:729
  164.9 43.4 %collective-permute-start.30 = (bf16[3,2,256,256]{3,2,1,0:T(8,128)(2,1)}, bf16[3,2,256,256]{3,2,1,0:T(8,128)(2,1)}, u32[]{:S(2)}, u32[]{:S(2)}) collective-permute-start(bf16[3,2,256,256]{3,2,1,0:T(8,128)(2,1)} %get-tuple-element.61), channel_id=1, source_target_pairs={{6,30},{12,20},{22,14},{28,4}} | collective-permute-start | bytes 2359304 | tf_op jit(solution)/shard_map/ppermute | solution.py:729
  166.2 12.6 %collective-permute-start.23 = (bf16[3,256,256]{2,1,0:T(8,128)(2,1)}, bf16[3,256,256]{2,1,0:T(8,128)(2,1)}, u32[]{:S(2)}, u32[]{:S(2)}) collective-permute-start(bf16[3,256,256]{2,1,0:T(8,128)(2,1)} %get-tuple-element.55.refs_0_), channel_id=1, source_target_pairs={{0,20},{1,29},{5,25},{6,2},{10,30},{11,7},{12,8},{15,3},{16,4},{17... | collective-permute-start | bytes 1179656 | tf_op jit(solution)/shard_map/ppermute | solution.py:729
  167.5 42.1 %collective-permute-start.31 = (bf16[3,2,256,256]{3,2,1,0:T(8,128)(2,1)}, bf16[3,2,256,256]{3,2,1,0:T(8,128)(2,1)}, u32[]{:S(2)}, u32[]{:S(2)}) collective-permute-start(bf16[3,2,256,256]{3,2,1,0:T(8,128)(2,1)} %get-tuple-element.61), channel_id=1, source_target_pairs={{2,30},{8,20},{18,14},{24,4}} | collective-permute-start | bytes 2359304 | tf_op jit(solution)/shard_map/ppermute | solution.py:729
  168.8 51.7 %collective-permute-start.25 = (bf16[3,2,256,256]{3,2,1,0:T(8,128)(2,1)}, bf16[3,2,256,256]{3,2,1,0:T(8,128)(2,1)}, u32[]{:S(2)}, u32[]{:S(2)}) collective-permute-start(bf16[3,2,256,256]{3,2,1,0:T(8,128)(2,1)} %get-tuple-element.58), channel_id=1, source_target_pairs={{4,20},{14,30},{20,4},{30,14}} | collective-permute-start | bytes 2359304 | tf_op jit(solution)/shard_map/ppermute | solution.py:729
  171.3 49.3 %collective-permute-start.26 = (bf16[3,2,256,256]{3,2,1,0:T(8,128)(2,1)}, bf16[3,2,256,256]{3,2,1,0:T(8,128)(2,1)}, u32[]{:S(2)}, u32[]{:S(2)}) collective-permute-start(bf16[3,2,256,256]{3,2,1,0:T(8,128)(2,1)} %get-tuple-element.58), channel_id=1, source_target_pairs={{0,20},{10,30},{16,4},{26,14}} | collective-permute-start | bytes 2359304 | tf_op jit(solution)/shard_map/ppermute | solution.py:729
  178.8 46.0 %collective-permute-start.34 = (bf16[3,2,256,256]{3,2,1,0:T(8,128)(2,1)}, bf16[3,2,256,256]{3,2,1,0:T(8,128)(2,1)}, u32[]{:S(2)}, u32[]{:S(2)}) collective-permute-start(bf16[3,2,256,256]{3,2,1,0:T(8,128)(2,1)} %collective-permute-done.24.refs_8_), channel_id=1, source_target_pairs={{2,30},{7,3},{8,4},{13,9},{18,14},{23,19},{24,20},{29,25}} | collective-permute-start | bytes 2359304 | tf_op jit(solution)/shard_map/ppermute | solution.py:729
  208.3 16.5 %collective-permute-start.32 = (bf16[3,256,256]{2,1,0:T(8,128)(2,1)}, bf16[3,256,256]{2,1,0:T(8,128)(2,1)}, u32[]{:S(2)}, u32[]{:S(2)}) collective-permute-start(bf16[3,256,256]{2,1,0:T(8,128)(2,1)} %get-tuple-element.57.refs_0_), channel_id=1, source_target_pairs={{2,3},{7,4},{8,9},{13,14},{18,19},{23,20},{24,25},{29,30}} | collective-permute-start | bytes 1179656 | tf_op jit(solution)/shard_map/ppermute | solution.py:729
  209.6 15.2 %collective-permute-start.33 = (bf16[3,256,256]{2,1,0:T(8,128)(2,1)}, bf16[3,256,256]{2,1,0:T(8,128)(2,1)}, u32[]{:S(2)}, u32[]{:S(2)}) collective-permute-start(bf16[3,256,256]{2,1,0:T(8,128)(2,1)} %get-tuple-element.57.refs_0_), channel_id=1, source_target_pairs={{2,30},{7,3},{8,4},{13,9},{18,14},{23,19},{24,20},{29,25}} | collective-permute-start | bytes 1179656 | tf_op jit(solution)/shard_map/ppermute | solution.py:729
where the time goes:
time: 233 us; the launch traced here: 232 us
  waiting for transfers between devices  127 us (55%)
  starting transfers between devices  52.8 us (23%)
  Pallas kernels  43.9 us (19%)
  local copies, waits for them, and re-layouts  5.98 us (3%)
    ppermute x35, waiting for transfers between devices, send(): return lax.ppermute(block, ('row', 'col'), routes)  127 us
    ppermute x35, starting transfers between devices, send(): return lax.ppermute(block, ('row', 'col'), routes)  52.8 us
    pallas_call x2, Pallas kernels, pack(): pl.pallas_call(kernel, in_specs=[place_spec(), any_spec(), any_spec()], o...  11.6 us
    pallas_call x2, Pallas kernels, sum_base(): pl.pallas_call(kernel, in_specs=[place_spec()] + [any_spec()] * (n_rows +...  10.6 us
    pallas_call x4, Pallas kernels, solve_stage(): pl.pallas_call(kernel, in_specs=[place_spec()] + [any_spec()] * (n_in - 1...  9.58 us
    pallas_call x1, Pallas kernels, copy_blocks(): pl.pallas_call(kernel, grid=(block_rows,), in_specs=[spec], out_specs=spe...  7.1 us
    pallas_call x2, Pallas kernels, sum_rest(): pl.pallas_call(kernel, in_specs=[place_spec()] + [any_spec()] * (n_cols +...  4.97 us
  transfers between devices with their start and end apart: 35, of which 16 were waited for; matrix products, arithmetic and copies ran while one was open for 3% of the time, Pallas kernels for 13%

commit v1 on v0

--- a/solution.py
+++ b/solution.py
@@ -192,7 +192,7 @@
     return output[:, None, :, None]
 
 
-ROUNDS = {0: [[(0, 1)]], 1: [[(1, 2), (0, 3)], [(0, 2), (1, 3)]], 2: [[(2, 3)]]}
+ROUNDS = {0: [[(0, 1)], [(0, 2)]], 1: [[(1, 2), (0, 3)], [(1, 3)]], 2: [[(2, 3)]]}
 
 
 def lag_of(r, c, cols):
@@ -574,7 +574,7 @@
 
     def kernel(place, out_in, *refs):
         refs = refs[len(passed) :]
-        group_refs, refs = refs[: len(flat)], refs[len(flat) :]
+        sum_groups, refs = refs[: len(flat)], refs[len(flat) :]
         row_in, refs = refs[:n_new], refs[n_new:]
         col_in, refs = refs[:n_new], refs[n_new:]
         pair_far, pair_own, space_in, out, sent, refs = *refs[:5], refs[5:]
@@ -593,27 +593,37 @@
                 sem += 1
                 return copy
 
-            small = []
+            news = []
             for n in range(n_new):
-                small.append(plan(row_in[n], row_buf.at[n]))
-                small.append(plan(col_in[n], col_buf.at[n]))
-            ours = plan(pair_own.at[pl.ds(0, count)], own_buf)
-            small += [plan(pair_far, far_buf), plan(space_in, space)]
-            targets = [total] + ([keep_r, keep_c] if n_new else [])
+                news.append(plan(row_in[n], row_buf.at[n]))
+                news.append(plan(col_in[n], col_buf.at[n]))
+            rest = [
+                plan(pair_own.at[pl.ds(0, count)], own_buf),
+                plan(pair_far, far_buf),
+                plan(space_in, space),
+            ]
+            near = pl.ds(0, max(stage, 1))
+            targets = [(0, total)]
+            if n_new:
+                targets += [(1, keep_r.at[:, near]), (2, keep_c.at[:, near])]
             first_sem = sem
-            for at, group in enumerate([group_refs[:3], group_refs[3:]][: len(groups)]):
+
+            def load(group, i, dst):
+                src = group[i].at[:, near] if i else group[i]
+                return pltpu.make_async_copy(src, dst, sems.at[first_sem + i])
+
+            for at, group in enumerate([sum_groups[:3], sum_groups[3:]][: len(groups)]):
                 chosen = is_late if at == 1 else jnp.logical_not(is_late)
-                for i, dst in enumerate(targets):
-                    copy = pltpu.make_async_copy(group[i], dst, sems.at[first_sem + i])
+                for i, dst in targets:
                     if two:
-                        pl.when(chosen)(copy.start)
+                        pl.when(chosen)(load(group, i, dst).start)
                     else:
-                        copy.start()
-            for copy in small + [ours]:
+                        load(group, i, dst).start()
+            for copy in news + rest:
                 copy.start()
-            for i, dst in enumerate(targets):
-                pltpu.make_async_copy(group_refs[i], dst, sems.at[first_sem + i]).wait()
-            for copy in small + [ours]:
+            for i, dst in targets:
+                load(sum_groups, i, dst).wait()
+            for copy in news:
                 copy.wait()
             lead = lead_of(r, c, cols)
             wrapped = jnp.where(r + lag >= rows, 1, 0)
@@ -626,6 +636,8 @@
                     right[a] = right[a] + mm(row_buf[n, a], keep_c[a, g - 1])
                     right[a] = right[a] - mm(keep_r[a, g - 1], col_buf[n, at])
             far = [jnp.minimum(a + wrapped, count - 1) for a in each]
+            for copy in rest:
+                copy.wait()
 
             def from_left(side, values):
                 left = [halves(own_buf[a, side]) for a in each]
@@ -759,9 +771,9 @@
     own_ids = jnp.arange(count, dtype=jnp.int32) * rows + r
     far_ids = jnp.minimum(own_ids + FIRST + lag_here, eigenvalues.shape[0] - 1)
     spacing = eigenvalues[own_ids][:, :, None] - eigenvalues[far_ids][:, None, :]
-    spacing = lax.optimization_barrier((spacing, own_far))[0]
+    known_later, spacing = lax.optimization_barrier((known, spacing))
     late_packs = pack(known, schur, place, 1, rows, cols, False)
-    output = copy_blocks(known)
+    output = copy_blocks(known_later)
 
     crossed = {n: send(early[n], lambda i, j: (i ^ 1, j)) for n in range(chips)}
     late = [(late_packs[0], 0, False)]
@@ -774,7 +786,7 @@
         def onward_across(i, j, onward=onward):
             return onward(i, j)[0] ^ 1, j
 
-        into = late_last if step == chips // 2 else late
+        into = late_last if step else late
         if step:
             into.append((send(late_packs[step], onward, late_core), step, False))
         into.append((send(late_packs[step], onward_across, late_core), step, True))

time: 233 us -> 241 us (1.034)
  the two profiles are of different devices: /device:TPU:17 before, /device:TPU:29 now
where the time goes in v1:
time: 241 us; the launch traced here: 240 us
  waiting for transfers between devices  144 us (60%)
  Pallas kernels  44.6 us (19%)
  starting transfers between devices  43.6 us (18%)
  local copies, waits for them, and re-layouts  5.92 us (2%)
    ppermute x37, waiting for transfers between devices, send(): return lax.ppermute(block, ('row', 'col'), routes)  144 us
    ppermute x37, starting transfers between devices, send(): return lax.ppermute(block, ('row', 'col'), routes)  43.6 us
    pallas_call x2, Pallas kernels, pack(): pl.pallas_call(kernel, in_specs=[place_spec(), any_spec(), any_spec()], o...  11.7 us
    pallas_call x2, Pallas kernels, sum_base(): pl.pallas_call(kernel, in_specs=[place_spec()] + [any_spec()] * (n_rows +...  9.2 us
    pallas_call x4, Pallas kernels, solve_stage(): pl.pallas_call(kernel, in_specs=[place_spec()] + [any_spec()] * (n_in - 1...  8.92 us
    pallas_call x2, Pallas kernels, sum_rest(): pl.pallas_call(kernel, in_specs=[place_spec()] + [any_spec()] * (n_cols +...  7.66 us
    pallas_call x1, Pallas kernels, copy_blocks(): pl.pallas_call(kernel, grid=(block_rows,), in_specs=[spec], out_specs=spe...  7.1 us
  transfers between devices with their start and end apart: 37, of which 17 were waited for; matrix products, arithmetic and copies ran while one was open for 3% of the time, Pallas kernels for 13%

profile of v1, /device:TPU:29, one launch (start us, length us, event | category | flops | bytes accessed | tf_op | source)
XLA Modules:
  0.0 239.9 jit_solution(13581623541716956694)
XLA Ops:
  0.6 6.8 %pack_first.1 = (bf16[3,2,256,256]{3,2,1,0:T(8,128)(2,1)}, bf16[3,2,256,256]{3,2,1,0:T(8,128)(2,1)}, bf16[3,2,256,256]{3,2,1,0:T(8,128)(2,1)}, bf16[3,2,256,256]...) custom-call(s32[2]{0:T(128)} %pad_add_fusion.place, ...), custom_call_target="tpu_custom_call" | custom-call | flops 235929600 | bytes 11796480 | tf_op jit(solution)/shard_map/pack_first/pallas_call | solution.py:307
  7.3 1.3 collective-permute-start.13
  8.6 1.3 collective-permute-start.14
  10.0 2.6 %collective-permute-start.5 = (bf16[3,2,256,256]{3,2,1,0:T(8,128)(2,1)}, bf16[3,2,256,256]{3,2,1,0:T(8,128)(2,1)}, u32[]{:S(2)}, u32[]{:S(2)}) collective-permute-start(bf16[3,2,256,256]{3,2,1,0:T(8,128)(2,1)} %get-tuple-element.41.refs_1_), channel_id=1, source_target_pairs={{0,2},{1,3},{2,0},{3,1},{4,6},{5,7},{6,4},{7,5},{8,10},{9,11},{10,... | collective-permute-start | bytes 2359304 | tf_op jit(solution)/shard_map/ppermute | solution.py:741
  13.6 5.4 %collective-permute-done.13.refs_15_.refs_11_ = bf16[3,256,256]{2,1,0:T(8,128)(2,1)S(1)} collective-permute-done((bf16[3,256,256]{2,1,0:T(8,128)(2,1)}, bf16[3,256,256]{2,1,0:T(8,128)(2,1)S(1)}, u32[]{:S(2)}, u32[]{:S(2)}) %collective-permute-start.13) | collective-permute-done | bytes 393248 | tf_op jit(solution)/shard_map/ppermute | solution.py:741
  18.9 1.3 collective-permute-start.15
  20.2 4.9 %collective-permute-done.14.refs_16_.refs_12_ = bf16[3,256,256]{2,1,0:T(8,128)(2,1)S(1)} collective-permute-done((bf16[3,256,256]{2,1,0:T(8,128)(2,1)}, bf16[3,256,256]{2,1,0:T(8,128)(2,1)S(1)}, u32[]{:S(2)}, u32[]{:S(2)}) %collective-permute-start.14) | collective-permute-done | bytes 393248 | tf_op jit(solution)/shard_map/ppermute | solution.py:741
  25.2 1.3 collective-permute-start.16
  26.5 3.7 %collective-permute-done.15.refs_17_.refs_13_ = bf16[3,256,256]{2,1,0:T(8,128)(2,1)S(1)} collective-permute-done((bf16[3,256,256]{2,1,0:T(8,128)(2,1)}, bf16[3,256,256]{2,1,0:T(8,128)(2,1)S(1)}, u32[]{:S(2)}, u32[]{:S(2)}) %collective-permute-start.15) | collective-permute-done | bytes 393248 | tf_op jit(solution)/shard_map/ppermute | solution.py:741
  30.2 5.5 %collective-permute-done.16.refs_18_.refs_14_ = bf16[3,256,256]{2,1,0:T(8,128)(2,1)S(1)} collective-permute-done((bf16[3,256,256]{2,1,0:T(8,128)(2,1)}, bf16[3,256,256]{2,1,0:T(8,128)(2,1)S(1)}, u32[]{:S(2)}, u32[]{:S(2)}) %collective-permute-start.16) | collective-permute-done | bytes 393248 | tf_op jit(solution)/shard_map/ppermute | solution.py:741
  35.7 3.3 %collective-permute-start.11 = (bf16[3,2,256,256]{3,2,1,0:T(8,128)(2,1)}, bf16[3,2,256,256]{3,2,1,0:T(8,128)(2,1)}, u32[]{:S(2)}, u32[]{:S(2)}) collective-permute-start(bf16[3,2,256,256]{3,2,1,0:T(8,128)(2,1)} %get-tuple-element.44), channel_id=1, source_target_pairs={{0,8},{1,9},{2,10},{3,11},{4,12},{5,13},{6,14},{7,15},{8,16},{9,17... | collective-permute-start | bytes 2359304 | tf_op jit(solution)/shard_map/ppermute | solution.py:741
  39.0 3.1 %collective-permute-done.5.refs_5_ = bf16[3,2,256,256]{3,2,1,0:T(8,128)(2,1)} collective-permute-done((bf16[3,2,256,256]{3,2,1,0:T(8,128)(2,1)}, bf16[3,2,256,256]{3,2,1,0:T(8,128)(2,1)}, u32[]{:S(2)}, u32[]{:S(2)}) %collective-permute-start.5) | collective-permute-done | bytes 786464 | tf_op jit(solution)/shard_map/ppermute | solution.py:741
  42.0 4.5 %collective-permute-done.3.refs_3_ = bf16[3,2,256,256]{3,2,1,0:T(8,128)(2,1)S(1)} collective-permute-done((bf16[3,2,256,256]{3,2,1,0:T(8,128)(2,1)}, bf16[3,2,256,256]{3,2,1,0:T(8,128)(2,1)S(1)}, u32[]{:S(2)}, u32[]{:S(2)}) %collective-permute-start.3) | collective-permute-done | bytes 786464 | tf_op jit(solution)/shard_map/ppermute | solution.py:741
  46.6 8.7 %collective-permute-done.4.refs_4_ = bf16[3,2,256,256]{3,2,1,0:T(8,128)(2,1)S(1)} collective-permute-done((bf16[3,2,256,256]{3,2,1,0:T(8,128)(2,1)}, bf16[3,2,256,256]{3,2,1,0:T(8,128)(2,1)S(1)}, u32[]{:S(2)}, u32[]{:S(2)}) %collective-permute-start.4) | collective-permute-done | bytes 786464 | tf_op jit(solution)/shard_map/ppermute | solution.py:741
  55.3 1.8 collective-permute-done.9.refs_10_
  57.1 14.7 %collective-permute-done.11.refs_12_ = bf16[3,2,256,256]{3,2,1,0:T(8,128)(2,1)} collective-permute-done((bf16[3,2,256,256]{3,2,1,0:T(8,128)(2,1)}, bf16[3,2,256,256]{3,2,1,0:T(8,128)(2,1)}, u32[]{:S(2)}, u32[]{:S(2)}) %collective-permute-start.11) | collective-permute-done | bytes 786464 | tf_op jit(solution)/shard_map/ppermute | solution.py:741
  72.4 33.1 %collective-permute-done.refs_0_ = bf16[3,2,256,256]{3,2,1,0:T(8,128)(2,1)} collective-permute-done((bf16[3,2,256,256]{3,2,1,0:T(8,128)(2,1)}, bf16[3,2,256,256]{3,2,1,0:T(8,128)(2,1)}, u32[]{:S(2)}, u32[]{:S(2)}) %collective-permute-start) | collective-permute-done | bytes 786464 | tf_op jit(solution)/shard_map/ppermute | solution.py:741
  106.1 1.3 gather_fusion
  107.4 1.3 gather_fusion.1
  109.8 2.4 slice.11.refs_3_
  113.1 1.6 collective-permute-start.19
  114.6 7.1 %copy_known.1.out_in = f32[4,8,256,256]{3,2,1,0:T(8,128)} custom-call(f32[4,8,256,256]{3,2,1,0:T(8,128)} %bitcast.13), custom_call_target="tpu_custom_call" | custom-call | flops 2097152000 | bytes 16777216 | tf_op jit(solution)/shard_map/copy_known/pallas_call | solution.py:334
  124.3 1.4 collective-permute-start.17
  125.7 1.4 collective-permute-start.18
  127.2 1.4 collective-permute-start.20
  128.6 1.4 collective-permute-start.22
  130.0 4.9 %pack_late.1 = (bf16[3,2,256,256]{3,2,1,0:T(8,128)(2,1)}, bf16[3,2,256,256]{3,2,1,0:T(8,128)(2,1)}, bf16[3,2,256,256]{3,2,1,0:T(8,128)(2,1)}, bf16[3,2,256,256]{3,2,1,0:T(8,128)(2,1)}) custom-call(s32[2]{0:T(128)} %pad_add_fusion.place, f32[4,8,256,256]{3,2,1,0:T(8,128)} %bitcast.14, bf16[4,8,256,256]{3,2,1,0:T(8,128)(2,1)} %bitcast.21), custom_call_target="tpu_custom_call" | custom-call | flops 157286400 | bytes 7864320 | tf_op jit(solution)/shard_map/pack_late/pallas_call | solution.py:307
  134.9 1.3 collective-permute-start.31
  136.3 1.3 collective-permute-start.25
  137.6 1.3 collective-permute-start.26
  138.9 1.6 collective-permute-start.24
  141.2 1.3 collective-permute-start.21
  142.5 13.9 %collective-permute-done.31.refs_9_ = bf16[3,2,256,256]{3,2,1,0:T(8,128)(2,1)} collective-permute-done((bf16[3,2,256,256]{3,2,1,0:T(8,128)(2,1)}, bf16[3,2,256,256]{3,2,1,0:T(8,128)(2,1)}, u32[]{:S(2)}, u32[]{:S(2)}) %collective-permute-start.31) | collective-permute-done | bytes 786464 | tf_op jit(solution)/shard_map/ppermute | solution.py:741
  156.4 1.3 collective-permute-start.23
  157.7 4.5 %collective-permute-done.25.refs_0_ = bf16[3,2,256,256]{3,2,1,0:T(8,128)(2,1)} collective-permute-done((bf16[3,2,256,256]{3,2,1,0:T(8,128)(2,1)}, bf16[3,2,256,256]{3,2,1,0:T(8,128)(2,1)}, u32[]{:S(2)}, u32[]{:S(2)}) %collective-permute-start.25) | collective-permute-done | bytes 786464 | tf_op jit(solution)/shard_map/ppermute | solution.py:741
  162.1 1.3 collective-permute-start.32
  164.2 4.8 %collective-permute-start.27 = (bf16[3,2,256,256]{3,2,1,0:T(8,128)(2,1)}, bf16[3,2,256,256]{3,2,1,0:T(8,128)(2,1)}, u32[]{:S(2)}, u32[]{:S(2)}) collective-permute-start(bf16[3,2,256,256]{3,2,1,0:T(8,128)(2,1)} %get-tuple-element.61), channel_id=1, source_target_pairs={{4,20},{14,30},{20,4},{30,14}} | collective-permute-start | bytes 2359304 | tf_op jit(solution)/shard_map/ppermute | solution.py:741
  169.1 1.3 collective-permute-start.34
  170.4 1.3 collective-permute-start.28
  171.7 1.3 collective-permute-start.29
  173.1 1.3 collective-permute-start.30
  174.4 5.4 %collective-permute-done.34.refs_11_ = bf16[3,256,256]{2,1,0:T(8,128)(2,1)} collective-permute-done((bf16[3,256,256]{2,1,0:T(8,128)(2,1)}, bf16[3,256,256]{2,1,0:T(8,128)(2,1)}, u32[]{:S(2)}, u32[]{:S(2)}) %collective-permute-start.34) | collective-permute-done | bytes 393248 | tf_op jit(solution)/shard_map/ppermute | solution.py:741
  182.1 29.6 %collective-permute-done.27.refs_2_ = bf16[3,2,256,256]{3,2,1,0:T(8,128)(2,1)} collective-permute-done((bf16[3,2,256,256]{3,2,1,0:T(8,128)(2,1)}, bf16[3,2,256,256]{3,2,1,0:T(8,128)(2,1)}, u32[]{:S(2)}, u32[]{:S(2)}) %collective-permute-start.27) | collective-permute-done | bytes 786464 | tf_op jit(solution)/shard_map/ppermute | solution.py:741
  211.7 1.3 collective-permute-start.33
  212.9 3.9 %collective-permute-done.28.refs_3_ = bf16[3,2,256,256]{3,2,1,0:T(8,128)(2,1)} collective-permute-done((bf16[3,2,256,256]{3,2,1,0:T(8,128)(2,1)}, bf16[3,2,256,256]{3,2,1,0:T(8,128)(2,1)}, u32[]{:S(2)}, u32[]{:S(2)}) %collective-permute-start.28) | collective-permute-done | bytes 786464 | tf_op jit(solution)/shard_map/ppermute | solution.py:741
  218.1 8.2 %sum_late.1 = (f32[3,256,256]{2,1,0:T(8,128)}, bf16[3,3,256,256]{3,2,1,0:T(8,128)(2,1)}, bf16[3,3,256,256]{3,2,1,0:T(8,128)(2,1)}, bf16[3,12,256,256]{3,2,1,0:T(8,128)(2,1)}) custom-call(s32[2]{0:T(128)} %pad_add_fusion.place, bf16[3,2,256,256]{3,2,1,0:T(8,128)(2,1)} %get-tuple-element.40.refs_0_, bf16[3,2,256,256]{3,2,1,0:T(8,128)(2,1)} %get-tuple-element.41.refs_1_, ...), custom_call_target="tpu_custom_call" | custom-call | flops 1811939328 | bytes 15728640 | tf_op jit(solution)/shard_map/sum_late/pallas_call | solution.py:467
  226.3 7.0 %rest_late.1 = (f32[3,256,256]{2,1,0:T(8,128)}, bf16[3,3,256,256]{3,2,1,0:T(8,128)(2,1)}) custom-call(s32[2]{0:T(128)} %pad_add_fusion.place, bf16[3,2,256,256]{3,2,1,0:T(8,128)(2,1)} %collective-permute-done.25.refs_0_, bf16[3,2,256,256]{3,2,1,0:T(8,128)(2,1)} %collective-permute-done.26.refs_1_, ...), custom_call_target="tpu_custom_call", output_to_operand_aliasing={{0}: (7, {}), {1}: (8, {})} | custom-call | flops 402653184 | bytes 4718592 | tf_op jit(solution)/shard_map/rest_late/pallas_call | solution.py:533
  233.3 6.4 %shard_map.49 = (f32[4,8,256,256]{3,2,1,0:T(8,128)}, bf16[3,256,256]{2,1,0:T(8,128)(2,1)}) custom-call(s32[2]{0:T(128)} %pad_add_fusion.place, f32[4,8,256,256]{3,2,1,0:T(8,128)} %get-tuple-element.58.out_in, bf16[3,256,256]{2,1,0:T(8,128)(2,1)} %get-tuple-element.59.refs_0_, ...), custom_call_target="tpu_custom_call", output_to_operand_aliasing={{0}: (1, {}), {1}: (2, {})} | custom-call | flops 1207959552 | bytes 7864320 | tf_op jit(solution)/shard_map/pallas_call | solution.py:683
  (61 shorter events, 12.4 us)
Async XLA Ops:
  7.3 11.6 %collective-permute-start.13 = (bf16[3,256,256]{2,1,0:T(8,128)(2,1)}, bf16[3,256,256]{2,1,0:T(8,128)(2,1)S(1)}, u32[]{:S(2)}, u32[]{:S(2)}) collective-permute-start(bf16[3,256,256]{2,1,0:T(8,128)(2,1)} %get-tuple-element.45.refs_14_.refs_10_), channel_id=1, source_target_pairs={{1,2},{2,3},{6,7},{7,4},{8,9},{11,8},{12,13},{13,14},{17,18},{18,1... | collective-permute-start | bytes 1179656 | tf_op jit(solution)/shard_map/ppermute | solution.py:741
  8.6 16.5 %collective-permute-start.14 = (bf16[3,256,256]{2,1,0:T(8,128)(2,1)}, bf16[3,256,256]{2,1,0:T(8,128)(2,1)S(1)}, u32[]{:S(2)}, u32[]{:S(2)}) collective-permute-start(bf16[3,256,256]{2,1,0:T(8,128)(2,1)} %get-tuple-element.45.refs_14_.refs_10_), channel_id=1, source_target_pairs={{1,3},{6,4},{11,9},{12,14},{17,19},{22,20},{27,25},{28,30}} | collective-permute-start | bytes 1179656 | tf_op jit(solution)/shard_map/ppermute | solution.py:741
  9.9 25.7 %collective-permute-start.2 = (bf16[3,2,256,256]{3,2,1,0:T(8,128)(2,1)}, bf16[3,2,256,256]{3,2,1,0:T(8,128)(2,1)S(1)}, u32[]{:S(2)}, u32[]{:S(2)}) collective-permute-start(bf16[3,2,256,256]{3,2,1,0:T(8,128)(2,1)} %get-tuple-element.40.refs_0_), channel_id=1, source_target_pairs={{0,1},{1,0},{2,3},{3,2},{4,5},{5,4},{6,7},{7,6},{8,9},{9,8},{10,11... | collective-permute-start | bytes 2359304 | tf_op jit(solution)/shard_map/ppermute | solution.py:741
  10.0 32.0 %collective-permute-start.5 = (bf16[3,2,256,256]{3,2,1,0:T(8,128)(2,1)}, bf16[3,2,256,256]{3,2,1,0:T(8,128)(2,1)}, u32[]{:S(2)}, u32[]{:S(2)}) collective-permute-start(bf16[3,2,256,256]{3,2,1,0:T(8,128)(2,1)} %get-tuple-element.41.refs_1_), channel_id=1, source_target_pairs={{0,2},{1,3},{2,0},{3,1},{4,6},{5,7},{6,4},{7,5},{8,10},{9,11},{10,... | collective-permute-start | bytes 2359304 | tf_op jit(solution)/shard_map/ppermute | solution.py:741
  12.7 33.9 %collective-permute-start.3 = (bf16[3,2,256,256]{3,2,1,0:T(8,128)(2,1)}, bf16[3,2,256,256]{3,2,1,0:T(8,128)(2,1)S(1)}, u32[]{:S(2)}, u32[]{:S(2)}) collective-permute-start(bf16[3,2,256,256]{3,2,1,0:T(8,128)(2,1)} %get-tuple-element.41.refs_1_), channel_id=1, source_target_pairs={{0,1},{1,0},{2,3},{3,2},{4,5},{5,4},{6,7},{7,6},{8,9},{9,8},{10,11... | collective-permute-start | bytes 2359304 | tf_op jit(solution)/shard_map/ppermute | solution.py:741
  18.9 7.5 %copy-start.4 = (bf16[3,256,256]{2,1,0:T(8,128)(2,1)}, bf16[3,256,256]{2,1,0:T(8,128)(2,1)S(1)}, u32[]{:S(2)}) copy-start(bf16[3,256,256]{2,1,0:T(8,128)(2,1)S(1)} %collective-permute-done.13.refs_15_.refs_11_) | copy-start | bytes 1179652
  18.9 11.2 %collective-permute-start.15 = (bf16[3,256,256]{2,1,0:T(8,128)(2,1)}, bf16[3,256,256]{2,1,0:T(8,128)(2,1)S(1)}, u32[]{:S(2)}, u32[]{:S(2)}) collective-permute-start(bf16[3,256,256]{2,1,0:T(8,128)(2,1)} %get-tuple-element.45.refs_14_.refs_10_), channel_id=1, source_target_pairs={{1,29},{2,30},{6,2},{7,3},{8,4},{11,7},{12,8},{13,9},{17,13},{18,1... | collective-permute-start | bytes 1179656 | tf_op jit(solution)/shard_map/ppermute | solution.py:741
  25.2 1.3 copy-start.5
  25.2 10.5 %collective-permute-start.16 = (bf16[3,256,256]{2,1,0:T(8,128)(2,1)}, bf16[3,256,256]{2,1,0:T(8,128)(2,1)S(1)}, u32[]{:S(2)}, u32[]{:S(2)}) collective-permute-start(bf16[3,256,256]{2,1,0:T(8,128)(2,1)} %get-tuple-element.45.refs_14_.refs_10_), channel_id=1, source_target_pairs={{1,25},{6,30},{11,3},{12,4},{17,9},{22,14},{27,19},{28,20}} | collective-permute-start | bytes 1179656 | tf_op jit(solution)/shard_map/ppermute | solution.py:741
  30.2 26.9 %copy-start.6 = (bf16[3,256,256]{2,1,0:T(8,128)(2,1)}, bf16[3,256,256]{2,1,0:T(8,128)(2,1)S(1)}, u32[]{:S(2)}) copy-start(bf16[3,256,256]{2,1,0:T(8,128)(2,1)S(1)} %collective-permute-done.15.refs_17_.refs_13_) | copy-start | bytes 1179652
  30.2 25.1 %collective-permute-start.4 = (bf16[3,2,256,256]{3,2,1,0:T(8,128)(2,1)}, bf16[3,2,256,256]{3,2,1,0:T(8,128)(2,1)S(1)}, u32[]{:S(2)}, u32[]{:S(2)}) collective-permute-start(bf16[3,2,256,256]{3,2,1,0:T(8,128)(2,1)} %get-tuple-element.40.refs_0_), channel_id=1, source_target_pairs={{0,2},{1,3},{2,0},{3,1},{4,6},{5,7},{6,4},{7,5},{8,10},{9,11},{10,... | collective-permute-start | bytes 2359304 | tf_op jit(solution)/shard_map/ppermute | solution.py:741
  35.7 36.2 %copy-start.7 = (bf16[3,256,256]{2,1,0:T(8,128)(2,1)}, bf16[3,256,256]{2,1,0:T(8,128)(2,1)S(1)}, u32[]{:S(2)}) copy-start(bf16[3,256,256]{2,1,0:T(8,128)(2,1)S(1)} %collective-permute-done.16.refs_18_.refs_14_) | copy-start | bytes 1179652
  35.7 21.4 %collective-permute-start.9 = (bf16[3,2,256,256]{3,2,1,0:T(8,128)(2,1)}, bf16[3,2,256,256]{3,2,1,0:T(8,128)(2,1)}, u32[]{:S(2)}, u32[]{:S(2)}) collective-permute-start(bf16[3,2,256,256]{3,2,1,0:T(8,128)(2,1)} %get-tuple-element.43), channel_id=1, source_target_pairs={{0,24},{1,25},{2,26},{3,27},{4,28},{5,29},{6,30},{7,31},{8,0},{9,1... | collective-permute-start | bytes 2359304 | tf_op jit(solution)/shard_map/ppermute | solution.py:741
  35.7 19.6 %copy-start = (bf16[3,2,256,256]{3,2,1,0:T(8,128)(2,1)}, bf16[3,2,256,256]{3,2,1,0:T(8,128)(2,1)S(1)}, u32[]{:S(2)}) copy-start(bf16[3,2,256,256]{3,2,1,0:T(8,128)(2,1)S(1)} %collective-permute-done.2.refs_2_) | copy-start | bytes 2359300
  35.7 36.2 %collective-permute-start.11 = (bf16[3,2,256,256]{3,2,1,0:T(8,128)(2,1)}, bf16[3,2,256,256]{3,2,1,0:T(8,128)(2,1)}, u32[]{:S(2)}, u32[]{:S(2)}) collective-permute-start(bf16[3,2,256,256]{3,2,1,0:T(8,128)(2,1)} %get-tuple-element.44), channel_id=1, source_target_pairs={{0,8},{1,9},{2,10},{3,11},{4,12},{5,13},{6,14},{7,15},{8,16},{9,17... | collective-permute-start | bytes 2359304 | tf_op jit(solution)/shard_map/ppermute | solution.py:741
  42.0 30.3 %collective-permute-start.8 = (bf16[3,2,256,256]{3,2,1,0:T(8,128)(2,1)}, bf16[3,2,256,256]{3,2,1,0:T(8,128)(2,1)}, u32[]{:S(2)}, u32[]{:S(2)}) collective-permute-start(bf16[3,2,256,256]{3,2,1,0:T(8,128)(2,1)} %get-tuple-element.42.refs_8_), channel_id=1, source_target_pairs={{0,4},{1,5},{2,6},{3,7},{4,0},{5,1},{6,2},{7,3},{8,12},{9,13},{10,... | collective-permute-start | bytes 2359304 | tf_op jit(solution)/shard_map/ppermute | solution.py:741
  46.6 8.8 %copy-start.1 = (bf16[3,2,256,256]{3,2,1,0:T(8,128)(2,1)}, bf16[3,2,256,256]{3,2,1,0:T(8,128)(2,1)S(1)}, u32[]{:S(2)}) copy-start(bf16[3,2,256,256]{3,2,1,0:T(8,128)(2,1)S(1)} %collective-permute-done.3.refs_3_) | copy-start | bytes 2359300
  46.6 59.0 %collective-permute-start = (bf16[3,2,256,256]{3,2,1,0:T(8,128)(2,1)}, bf16[3,2,256,256]{3,2,1,0:T(8,128)(2,1)}, u32[]{:S(2)}, u32[]{:S(2)}) collective-permute-start(bf16[3,2,256,256]{3,2,1,0:T(8,128)(2,1)} %get-tuple-element.39), channel_id=1, source_target_pairs={{0,16},{1,17},{2,18},{3,19},{4,20},{5,21},{6,22},{7,23},{8,24},{9,... | collective-permute-start | bytes 2359304 | tf_op jit(solution)/shard_map/ppermute | solution.py:741
  55.3 1.8 copy-start.2
  55.3 56.9 %collective-permute-start.6 = (bf16[3,2,256,256]{3,2,1,0:T(8,128)(2,1)S(1)}, bf16[3,2,256,256]{3,2,1,0:T(8,128)(2,1)S(1)}, u32[]{:S(2)}, u32[]{:S(2)}) collective-permute-start(bf16[3,2,256,256]{3,2,1,0:T(8,128)(2,1)S(1)} %collective-permute-done.2.refs_2_), channel_id=1, source_target_pairs={{0,2},{1,3},{2,0},{3,1},{4,6},{5,7},{6,4},{7,5},{8,10},{9,11},{10,... | collective-permute-start | bytes 2359304 | tf_op jit(solution)/shard_map/ppermute | solution.py:741
  57.1 64.6 %collective-permute-start.7 = (bf16[3,2,256,256]{3,2,1,0:T(8,128)(2,1)}, bf16[3,2,256,256]{3,2,1,0:T(8,128)(2,1)}, u32[]{:S(2)}, u32[]{:S(2)}) collective-permute-start(bf16[3,2,256,256]{3,2,1,0:T(8,128)(2,1)} %collective-permute-done.5.refs_5_), channel_id=1, source_target_pairs={{0,1},{1,0},{2,3},{3,2},{4,5},{5,4},{6,7},{7,6},{8,9},{9,8},{10,11... | collective-permute-start | bytes 2359304 | tf_op jit(solution)/shard_map/ppermute | solution.py:741
  71.9 49.9 %collective-permute-start.10 = (bf16[3,2,256,256]{3,2,1,0:T(8,128)(2,1)}, bf16[3,2,256,256]{3,2,1,0:T(8,128)(2,1)}, u32[]{:S(2)}, u32[]{:S(2)}) collective-permute-start(bf16[3,2,256,256]{3,2,1,0:T(8,128)(2,1)} %collective-permute-done.9.refs_10_), channel_id=1, source_target_pairs={{0,4},{1,5},{2,6},{3,7},{4,0},{5,1},{6,2},{7,3},{8,12},{9,13},{10,... | collective-permute-start | bytes 2359304 | tf_op jit(solution)/shard_map/ppermute | solution.py:741
  72.4 49.4 %collective-permute-start.12 = (bf16[3,2,256,256]{3,2,1,0:T(8,128)(2,1)}, bf16[3,2,256,256]{3,2,1,0:T(8,128)(2,1)}, u32[]{:S(2)}, u32[]{:S(2)}) collective-permute-start(bf16[3,2,256,256]{3,2,1,0:T(8,128)(2,1)} %collective-permute-done.11.refs_12_), channel_id=1, source_target_pairs={{0,4},{1,5},{2,6},{3,7},{4,0},{5,1},{6,2},{7,3},{8,12},{9,13},{10,... | collective-permute-start | bytes 2359304 | tf_op jit(solution)/shard_map/ppermute | solution.py:741
  105.6 17.2 %collective-permute-start.1 = (bf16[3,2,256,256]{3,2,1,0:T(8,128)(2,1)}, bf16[3,2,256,256]{3,2,1,0:T(8,128)(2,1)}, u32[]{:S(2)}, u32[]{:S(2)}) collective-permute-start(bf16[3,2,256,256]{3,2,1,0:T(8,128)(2,1)} %collective-permute-done.refs_0_), channel_id=1, source_target_pairs={{0,4},{1,5},{2,6},{3,7},{4,0},{5,1},{6,2},{7,3},{8,12},{9,13},{10,... | collective-permute-start | bytes 2359304 | tf_op jit(solution)/shard_map/ppermute | solution.py:741
  112.2 0.9 copy-start.3
  113.1 21.9 %collective-permute-start.19 = (bf16[3,2,256,256]{3,2,1,0:T(8,128)(2,1)}, bf16[3,2,256,256]{3,2,1,0:T(8,128)(2,1)}, u32[]{:S(2)}, u32[]{:S(2)}) collective-permute-start(bf16[3,2,256,256]{3,2,1,0:T(8,128)(2,1)} %slice.11.refs_3_), channel_id=1, source_target_pairs={{0,28},{5,1},{10,6},{15,11},{16,12},{21,17},{26,22},{31,27}} | collective-permute-start | bytes 2359304 | tf_op jit(solution)/shard_map/ppermute | solution.py:741
  124.3 12.0 %collective-permute-start.17 = (bf16[3,256,256]{2,1,0:T(8,128)(2,1)}, bf16[3,256,256]{2,1,0:T(8,128)(2,1)}, u32[]{:S(2)}, u32[]{:S(2)}) collective-permute-start(bf16[3,256,256]{2,1,0:T(8,128)(2,1)} %get-tuple-element.55.refs_0_), channel_id=1, source_target_pairs={{0,1},{5,6},{10,11},{15,12},{16,17},{21,22},{26,27},{31,28}} | collective-permute-start | bytes 1179656 | tf_op jit(solution)/shard_map/ppermute | solution.py:741
  125.7 11.8 %collective-permute-start.18 = (bf16[3,256,256]{2,1,0:T(8,128)(2,1)}, bf16[3,256,256]{2,1,0:T(8,128)(2,1)}, u32[]{:S(2)}, u32[]{:S(2)}) collective-permute-start(bf16[3,256,256]{2,1,0:T(8,128)(2,1)} %get-tuple-element.55.refs_0_), channel_id=1, source_target_pairs={{0,28},{5,1},{10,6},{15,11},{16,12},{21,17},{26,22},{31,27}} | collective-permute-start | bytes 1179656 | tf_op jit(solution)/shard_map/ppermute | solution.py:741
  127.2 11.7 %collective-permute-start.20 = (bf16[3,256,256]{2,1,0:T(8,128)(2,1)}, bf16[3,256,256]{2,1,0:T(8,128)(2,1)}, u32[]{:S(2)}, u32[]{:S(2)}) collective-permute-start(bf16[3,256,256]{2,1,0:T(8,128)(2,1)} %get-tuple-element.55.refs_0_), channel_id=1, source_target_pairs={{0,2},{5,7},{10,8},{15,13},{16,18},{21,23},{26,24},{31,29}} | collective-permute-start | bytes 1179656 | tf_op jit(solution)/shard_map/ppermute | solution.py:741
  128.6 11.8 %collective-permute-start.22 = (bf16[3,256,256]{2,1,0:T(8,128)(2,1)}, bf16[3,256,256]{2,1,0:T(8,128)(2,1)}, u32[]{:S(2)}, u32[]{:S(2)}) collective-permute-start(bf16[3,256,256]{2,1,0:T(8,128)(2,1)} %get-tuple-element.55.refs_0_), channel_id=1, source_target_pairs={{0,24},{5,29},{10,2},{15,7},{16,8},{21,13},{26,18},{31,23}} | collective-permute-start | bytes 1179656 | tf_op jit(solution)/shard_map/ppermute | solution.py:741
  134.9 21.4 %collective-permute-start.31 = (bf16[3,2,256,256]{3,2,1,0:T(8,128)(2,1)}, bf16[3,2,256,256]{3,2,1,0:T(8,128)(2,1)}, u32[]{:S(2)}, u32[]{:S(2)}) collective-permute-start(bf16[3,2,256,256]{3,2,1,0:T(8,128)(2,1)} %get-tuple-element.63.refs_8_), channel_id=1, source_target_pairs={{0,4},{10,14},{16,20},{26,30}} | collective-permute-start | bytes 2359304 | tf_op jit(solution)/shard_map/ppermute | solution.py:741
  136.3 25.9 %collective-permute-start.25 = (bf16[3,2,256,256]{3,2,1,0:T(8,128)(2,1)}, bf16[3,2,256,256]{3,2,1,0:T(8,128)(2,1)}, u32[]{:S(2)}, u32[]{:S(2)}) collective-permute-start(bf16[3,2,256,256]{3,2,1,0:T(8,128)(2,1)} %get-tuple-element.60), channel_id=1, source_target_pairs={{6,14},{12,4},{22,30},{28,20}} | collective-permute-start | bytes 2359304 | tf_op jit(solution)/shard_map/ppermute | solution.py:741
  137.6 26.6 %collective-permute-start.26 = (bf16[3,2,256,256]{3,2,1,0:T(8,128)(2,1)}, bf16[3,2,256,256]{3,2,1,0:T(8,128)(2,1)}, u32[]{:S(2)}, u32[]{:S(2)}) collective-permute-start(bf16[3,2,256,256]{3,2,1,0:T(8,128)(2,1)} %get-tuple-element.60), channel_id=1, source_target_pairs={{2,14},{8,4},{18,30},{24,20}} | collective-permute-start | bytes 2359304 | tf_op jit(solution)/shard_map/ppermute | solution.py:741
  138.9 30.2 %collective-permute-start.24 = (bf16[3,2,256,256]{3,2,1,0:T(8,128)(2,1)}, bf16[3,2,256,256]{3,2,1,0:T(8,128)(2,1)}, u32[]{:S(2)}, u32[]{:S(2)}) collective-permute-start(bf16[3,2,256,256]{3,2,1,0:T(8,128)(2,1)} %collective-permute-done.19.refs_6_), channel_id=1, source_target_pairs={{1,29},{6,2},{11,7},{12,8},{17,13},{22,18},{27,23},{28,24}} | collective-permute-start | bytes 2359304 | tf_op jit(solution)/shard_map/ppermute | solution.py:741
  141.2 29.2 %collective-permute-start.21 = (bf16[3,256,256]{2,1,0:T(8,128)(2,1)}, bf16[3,256,256]{2,1,0:T(8,128)(2,1)}, u32[]{:S(2)}, u32[]{:S(2)}) collective-permute-start(bf16[3,256,256]{2,1,0:T(8,128)(2,1)} %get-tuple-element.57.refs_0_), channel_id=1, source_target_pairs={{0,3},{1,2},{5,4},{6,7},{10,9},{11,8},{12,13},{15,14},{16,19},{17,... | collective-permute-start | bytes 1179656 | tf_op jit(solution)/shard_map/ppermute | solution.py:741
  156.4 15.3 %collective-permute-start.23 = (bf16[3,256,256]{2,1,0:T(8,128)(2,1)}, bf16[3,256,256]{2,1,0:T(8,128)(2,1)}, u32[]{:S(2)}, u32[]{:S(2)}) collective-permute-start(bf16[3,256,256]{2,1,0:T(8,128)(2,1)} %get-tuple-element.57.refs_0_), channel_id=1, source_target_pairs={{0,20},{1,29},{5,25},{6,2},{10,30},{11,7},{12,8},{15,3},{16,4},{17... | collective-permute-start | bytes 1179656 | tf_op jit(solution)/shard_map/ppermute | solution.py:741
  162.1 11.0 %collective-permute-start.32 = (bf16[3,256,256]{2,1,0:T(8,128)(2,1)}, bf16[3,256,256]{2,1,0:T(8,128)(2,1)}, u32[]{:S(2)}, u32[]{:S(2)}) collective-permute-start(bf16[3,256,256]{2,1,0:T(8,128)(2,1)} %get-tuple-element.57.refs_0_), channel_id=1, source_target_pairs={{1,3},{6,4},{11,9},{12,14},{17,19},{22,20},{27,25},{28,30}} | collective-permute-start | bytes 1179656 | tf_op jit(solution)/shard_map/ppermute | solution.py:741
  164.2 47.4 %collective-permute-start.27 = (bf16[3,2,256,256]{3,2,1,0:T(8,128)(2,1)}, bf16[3,2,256,256]{3,2,1,0:T(8,128)(2,1)}, u32[]{:S(2)}, u32[]{:S(2)}) collective-permute-start(bf16[3,2,256,256]{3,2,1,0:T(8,128)(2,1)} %get-tuple-element.61), channel_id=1, source_target_pairs={{4,20},{14,30},{20,4},{30,14}} | collective-permute-start | bytes 2359304 | tf_op jit(solution)/shard_map/ppermute | solution.py:741
  169.1 10.7 %collective-permute-start.34 = (bf16[3,256,256]{2,1,0:T(8,128)(2,1)}, bf16[3,256,256]{2,1,0:T(8,128)(2,1)}, u32[]{:S(2)}, u32[]{:S(2)}) collective-permute-start(bf16[3,256,256]{2,1,0:T(8,128)(2,1)} %get-tuple-element.57.refs_0_), channel_id=1, source_target_pairs={{1,25},{6,30},{11,3},{12,4},{17,9},{22,14},{27,19},{28,20}} | collective-permute-start | bytes 1179656 | tf_op jit(solution)/shard_map/ppermute | solution.py:741
  170.4 46.4 %collective-permute-start.28 = (bf16[3,2,256,256]{3,2,1,0:T(8,128)(2,1)}, bf16[3,2,256,256]{3,2,1,0:T(8,128)(2,1)}, u32[]{:S(2)}, u32[]{:S(2)}) collective-permute-start(bf16[3,2,256,256]{3,2,1,0:T(8,128)(2,1)} %get-tuple-element.61), channel_id=1, source_target_pairs={{0,20},{10,30},{16,4},{26,14}} | collective-permute-start | bytes 2359304 | tf_op jit(solution)/shard_map/ppermute | solution.py:741
  171.7 54.6 %collective-permute-start.29 = (bf16[3,2,256,256]{3,2,1,0:T(8,128)(2,1)}, bf16[3,2,256,256]{3,2,1,0:T(8,128)(2,1)}, u32[]{:S(2)}, u32[]{:S(2)}) collective-permute-start(bf16[3,2,256,256]{3,2,1,0:T(8,128)(2,1)} %get-tuple-element.62), channel_id=1, source_target_pairs={{6,30},{12,20},{22,14},{28,4}} | collective-permute-start | bytes 2359304 | tf_op jit(solution)/shard_map/ppermute | solution.py:741
  173.1 53.2 %collective-permute-start.30 = (bf16[3,2,256,256]{3,2,1,0:T(8,128)(2,1)}, bf16[3,2,256,256]{3,2,1,0:T(8,128)(2,1)}, u32[]{:S(2)}, u32[]{:S(2)}) collective-permute-start(bf16[3,2,256,256]{3,2,1,0:T(8,128)(2,1)} %get-tuple-element.62), channel_id=1, source_target_pairs={{2,30},{8,20},{18,14},{24,4}} | collective-permute-start | bytes 2359304 | tf_op jit(solution)/shard_map/ppermute | solution.py:741
  179.8 53.4 %collective-permute-start.36 = (bf16[3,2,256,256]{3,2,1,0:T(8,128)(2,1)}, bf16[3,2,256,256]{3,2,1,0:T(8,128)(2,1)}, u32[]{:S(2)}, u32[]{:S(2)}) collective-permute-start(bf16[3,2,256,256]{3,2,1,0:T(8,128)(2,1)} %collective-permute-done.24.refs_8_), channel_id=1, source_target_pairs={{2,30},{7,3},{8,4},{13,9},{18,14},{23,19},{24,20},{29,25}} | collective-permute-start | bytes 2359304 | tf_op jit(solution)/shard_map/ppermute | solution.py:741
  211.7 21.6 %collective-permute-start.33 = (bf16[3,256,256]{2,1,0:T(8,128)(2,1)}, bf16[3,256,256]{2,1,0:T(8,128)(2,1)}, u32[]{:S(2)}, u32[]{:S(2)}) collective-permute-start(bf16[3,256,256]{2,1,0:T(8,128)(2,1)} %get-tuple-element.59.refs_0_), channel_id=1, source_target_pairs={{2,3},{7,4},{8,9},{13,14},{18,19},{23,20},{24,25},{29,30}} | collective-permute-start | bytes 1179656 | tf_op jit(solution)/shard_map/ppermute | solution.py:741
  216.8 16.5 %collective-permute-start.35 = (bf16[3,256,256]{2,1,0:T(8,128)(2,1)}, bf16[3,256,256]{2,1,0:T(8,128)(2,1)}, u32[]{:S(2)}, u32[]{:S(2)}) collective-permute-start(bf16[3,256,256]{2,1,0:T(8,128)(2,1)} %get-tuple-element.59.refs_0_), channel_id=1, source_target_pairs={{2,30},{7,3},{8,4},{13,9},{18,14},{23,19},{24,20},{29,25}} | collective-permute-start | bytes 1179656 | tf_op jit(solution)/shard_map/ppermute | solution.py:741

commit v2 on v1

--- a/solution.py
+++ b/solution.py
@@ -229,15 +229,18 @@
     return lax.div(j - off_f - r, rows), lax.div(j - off_s - r, rows), (j - c) // cols
 
 
-def pack(known, schur, place, aim_core, rows, cols, first):
+def pack(known, schur, place, aim_core, rows, cols, kind):
     block_rows, block_cols, bs = known.shape[0], known.shape[1], known.shape[2]
     count = block_rows - 1
     chips = rows // 2
     slots = FIRST // cols
 
+    first = kind == "rows"
     n_rows = slots if first else 0
-    shapes = [(count, 2, bs, bs)] * (n_rows + chips) + ([(count, bs, bs)] if first else [])
-    total = count * (n_rows + chips)
+    n_cols = 0 if first else chips
+    shapes = [(count, 2, bs, bs)] * (n_rows + n_cols) + ([(count, bs, bs)] if first else [])
+    total = count * (n_rows + n_cols)
+    steps = [] if first else [x for x in range(1, chips) if x != chips // 2] + [chips // 2, 0]
 
     def kernel(place, known_ref, schur_ref, *refs):
         outs, refs = refs[: len(shapes)], refs[len(shapes) :]
@@ -246,10 +249,10 @@
         r, c = place[0], place[1]
         lead = lead_of(r, c, cols)
         groups = []
-        for step in [chips // 2] + [x for x in range(1, chips) if x != chips // 2] + [0]:
+        for step in steps:
             picks = []
             for a in range(count):
-                way = step if first else mirrored(step, c, cols)
+                way = mirrored(step, c, cols) if kind == "late" else step
                 f_row, s_row, b = column_picks(place, way, chips, aim_core, rows, cols, a)
                 picks.append(((f_row, b), (s_row, b)))
             groups.append((n_rows + step, picks))
@@ -259,7 +262,7 @@
             for a in range(count):
                 base = (rows // cols) * a + lead + slot
                 picks.append(((a, base), (a, base + extra)))
-            groups.insert(1 + slot, (slot, picks))
+            groups.append((slot, picks))
 
         def clip(at):
             return jnp.clip(at[0], 0, block_rows - 1), jnp.clip(at[1], 0, block_cols - 1)
@@ -320,7 +323,6 @@
         cost_estimate=pl.CostEstimate(
             flops=total * bs * bs * 200, bytes_accessed=total * bs * bs * 10, transcendentals=0
         ),
-        name="pack_first" if first else "pack_late",
     )(place, known, schur)
 
 
@@ -723,7 +725,6 @@
     pairs = eigen_pairs[:, 0]
     count = known.shape[0] - 1
     chips = rows // 2
-    slots = FIRST // cols
     devices = [(i, k) for i in range(rows) for k in range(cols)]
 
     def lag(i, k):
@@ -744,8 +745,9 @@
         return lag(i, k) == cols - 1 and i % 2 == 1
 
     place = jnp.stack([r, c]).astype(jnp.int32)
-    packed = pack(known, schur, place, 0, rows, cols, True)
-    own_parts, col_packs, own_far = packed[:slots], packed[slots:-1], packed[-1]
+    col_packs = pack(known, schur, place, 0, rows, cols, "cols")
+    packed = pack(known, schur, place, 0, rows, cols, "rows")
+    own_parts, own_far = packed[:-1], packed[-1]
     early = {0: col_packs[0]}
     for step in range(1, chips):
         early[step] = send(col_packs[step], lambda i, j, s=step: (i - 2 * s, j))
@@ -772,7 +774,7 @@
     far_ids = jnp.minimum(own_ids + FIRST + lag_here, eigenvalues.shape[0] - 1)
     spacing = eigenvalues[own_ids][:, :, None] - eigenvalues[far_ids][:, None, :]
     known_later, spacing = lax.optimization_barrier((known, spacing))
-    late_packs = pack(known, schur, place, 1, rows, cols, False)
+    late_packs = pack(known, schur, place, 1, rows, cols, "late")
     output = copy_blocks(known_later)
 
     crossed = {n: send(early[n], lambda i, j: (i ^ 1, j)) for n in range(chips)}

time: 241 us -> 241 us (level)
  waiting for transfers between devices: 144 us -> 139 us
  starting transfers between devices: 43.6 us -> 47.4 us
    ppermute x37, waiting for transfers between devices: 144 us -> 139 us  [send(): return lax.ppermute(block, ('row', 'col'), routes)]
    ppermute x37, starting transfers between devices: 43.6 us -> 47.4 us  [send(): return lax.ppermute(block, ('row', 'col'), routes)]
    pallas_call x2 -> x3, Pallas kernels: 11.7 us -> 13.6 us  [pack(): pl.pallas_call(kernel, in_specs=[place_spec(), any_spec(), any_spec()], o...]
  transfers between devices with their start and end apart: 37 -> 37, of which waited for: 17 -> 15; matrix products, arithmetic and copies ran while one was open for 3% -> 3% of each run, Pallas kernels for 13% -> 15%
where the time goes in v2:
time: 241 us; the launch traced here: 240 us
  waiting for transfers between devices  139 us (58%)
  starting transfers between devices  47.4 us (20%)
  Pallas kernels  46.5 us (19%)
  local copies, waits for them, and re-layouts  5.02 us (2%)
    ppermute x37, waiting for transfers between devices, send(): return lax.ppermute(block, ('row', 'col'), routes)  139 us
    ppermute x37, starting transfers between devices, send(): return lax.ppermute(block, ('row', 'col'), routes)  47.4 us
    pallas_call x3, Pallas kernels, pack(): pl.pallas_call(kernel, in_specs=[place_spec(), any_spec(), any_spec()], o...  13.6 us
    pallas_call x2, Pallas kernels, sum_base(): pl.pallas_call(kernel, in_specs=[place_spec()] + [any_spec()] * (n_rows +...  9.15 us
    pallas_call x4, Pallas kernels, solve_stage(): pl.pallas_call(kernel, in_specs=[place_spec()] + [any_spec()] * (n_in - 1...  8.92 us
    pallas_call x2, Pallas kernels, sum_rest(): pl.pallas_call(kernel, in_specs=[place_spec()] + [any_spec()] * (n_cols +...  7.67 us
    pallas_call x1, Pallas kernels, copy_blocks(): pl.pallas_call(kernel, grid=(block_rows,), in_specs=[spec], out_specs=spe...  7.1 us
  transfers between devices with their start and end apart: 37, of which 15 were waited for; matrix products, arithmetic and copies ran while one was open for 3% of the time, Pallas kernels for 15%

profile of v2, /device:TPU:29, one launch (start us, length us, event | category | flops | bytes accessed | tf_op | source)
XLA Modules:
  0.0 240.2 jit_solution(18310507939275973084)
XLA Ops:
  0.6 3.6 %shard_map.47 = (bf16[3,2,256,256]{3,2,1,0:T(8,128)(2,1)}, bf16[3,2,256,256]{3,2,1,0:T(8,128)(2,1)}, bf16[3,256,256]{2,1,0:T(8,128)(2,1)}) custom-call(s32[2]{0:T(128)} %pad_add_fusion.place, f32[4,8,256,256]{3,2,1,0:T(8,128)} %bitcast.12, bf16[4,8,256,256]{3,2,1,0:T(8,128)(2,1)} %bitcast.21), custom_call_target="tpu_custom_call" | custom-call | flops 78643200 | bytes 3932160 | tf_op jit(solution)/shard_map/pallas_call | solution.py:310
  4.2 1.3 collective-permute-start.13
  5.5 1.3 collective-permute-start.14
  6.8 1.5 collective-permute-start.2
  8.3 2.1 collective-permute-start.5
  10.3 1.5 collective-permute-start.3
  11.8 3.3 %collective-permute-done.13.refs_15_.refs_11_ = bf16[3,256,256]{2,1,0:T(8,128)(2,1)} collective-permute-done((bf16[3,256,256]{2,1,0:T(8,128)(2,1)}, bf16[3,256,256]{2,1,0:T(8,128)(2,1)}, u32[]{:S(2)}, u32[]{:S(2)}) %collective-permute-start.13) | collective-permute-done | bytes 393248 | tf_op jit(solution)/shard_map/ppermute | solution.py:742
  16.4 5.2 %collective-permute-done.14.refs_16_.refs_12_ = bf16[3,256,256]{2,1,0:T(8,128)(2,1)} collective-permute-done((bf16[3,256,256]{2,1,0:T(8,128)(2,1)}, bf16[3,256,256]{2,1,0:T(8,128)(2,1)}, u32[]{:S(2)}, u32[]{:S(2)}) %collective-permute-start.14) | collective-permute-done | bytes 393248 | tf_op jit(solution)/shard_map/ppermute | solution.py:742
  22.9 4.5 %collective-permute-done.15.refs_17_.refs_13_ = bf16[3,256,256]{2,1,0:T(8,128)(2,1)} collective-permute-done((bf16[3,256,256]{2,1,0:T(8,128)(2,1)}, bf16[3,256,256]{2,1,0:T(8,128)(2,1)}, u32[]{:S(2)}, u32[]{:S(2)}) %collective-permute-start.15) | collective-permute-done | bytes 393248 | tf_op jit(solution)/shard_map/ppermute | solution.py:742
  27.4 5.0 %shard_map.46 = (bf16[3,2,256,256]{3,2,1,0:T(8,128)(2,1)}, bf16[3,2,256,256]{3,2,1,0:T(8,128)(2,1)}, bf16[3,2,256,256]{3,2,1,0:T(8,128)(2,1)}, bf16[3,2,256,256]{3,2,1,0:T(8,128)(2,1)}) custom-call(s32[2]{0:T(128)} %pad_add_fusion.place, f32[4,8,256,256]{3,2,1,0:T(8,128)} %bitcast.13, bf16[4,8,256,256]{3,2,1,0:T(8,128)(2,1)} %bitcast.22), custom_call_target="tpu_custom_call" | custom-call | flops 157286400 | bytes 7864320 | tf_op jit(solution)/shard_map/pallas_call | solution.py:310
  32.5 4.2 %collective-permute-start.9 = (bf16[3,2,256,256]{3,2,1,0:T(8,128)(2,1)}, bf16[3,2,256,256]{3,2,1,0:T(8,128)(2,1)}, u32[]{:S(2)}, u32[]{:S(2)}) collective-permute-start(bf16[3,2,256,256]{3,2,1,0:T(8,128)(2,1)} %get-tuple-element.43), channel_id=1, source_target_pairs={{0,24},{1,25},{2,26},{3,27},{4,28},{5,29},{6,30},{7,31},{8,0},{9,1... | collective-permute-start | bytes 2359304 | tf_op jit(solution)/shard_map/ppermute | solution.py:742
  36.7 1.7 collective-permute-done.5.refs_5_
  39.1 4.1 %collective-permute-done.3.refs_3_ = bf16[3,2,256,256]{3,2,1,0:T(8,128)(2,1)} collective-permute-done((bf16[3,2,256,256]{3,2,1,0:T(8,128)(2,1)}, bf16[3,2,256,256]{3,2,1,0:T(8,128)(2,1)}, u32[]{:S(2)}, u32[]{:S(2)}) %collective-permute-start.3) | collective-permute-done | bytes 786464 | tf_op jit(solution)/shard_map/ppermute | solution.py:742
  43.3 8.8 %collective-permute-done.4.refs_4_ = bf16[3,2,256,256]{3,2,1,0:T(8,128)(2,1)} collective-permute-done((bf16[3,2,256,256]{3,2,1,0:T(8,128)(2,1)}, bf16[3,2,256,256]{3,2,1,0:T(8,128)(2,1)}, u32[]{:S(2)}, u32[]{:S(2)}) %collective-permute-start.4) | collective-permute-done | bytes 786464 | tf_op jit(solution)/shard_map/ppermute | solution.py:742
  52.1 2.3 collective-permute-done.9.refs_10_
  55.4 16.4 %collective-permute-done.11.refs_12_ = bf16[3,2,256,256]{3,2,1,0:T(8,128)(2,1)} collective-permute-done((bf16[3,2,256,256]{3,2,1,0:T(8,128)(2,1)}, bf16[3,2,256,256]{3,2,1,0:T(8,128)(2,1)}, u32[]{:S(2)}, u32[]{:S(2)}) %collective-permute-start.11) | collective-permute-done | bytes 786464 | tf_op jit(solution)/shard_map/ppermute | solution.py:742
  72.4 33.1 %collective-permute-done.refs_0_ = bf16[3,2,256,256]{3,2,1,0:T(8,128)(2,1)} collective-permute-done((bf16[3,2,256,256]{3,2,1,0:T(8,128)(2,1)}, bf16[3,2,256,256]{3,2,1,0:T(8,128)(2,1)}, u32[]{:S(2)}, u32[]{:S(2)}) %collective-permute-start) | collective-permute-done | bytes 786464 | tf_op jit(solution)/shard_map/ppermute | solution.py:742
  105.9 1.3 gather_fusion
  107.2 1.3 gather_fusion.1
  109.6 2.4 slice.11.refs_3_
  112.0 1.6 collective-permute-start.19
  113.6 7.1 %copy_known.1.out_in = f32[4,8,256,256]{3,2,1,0:T(8,128)} custom-call(f32[4,8,256,256]{3,2,1,0:T(8,128)} %bitcast.14), custom_call_target="tpu_custom_call" | custom-call | flops 2097152000 | bytes 16777216 | tf_op jit(solution)/shard_map/copy_known/pallas_call | solution.py:336
  123.2 1.4 collective-permute-start.17
  124.7 1.4 collective-permute-start.18
  126.1 1.5 collective-permute-start.20
  127.6 1.4 collective-permute-start.22
  129.0 5.0 %shard_map.51 = (bf16[3,2,256,256]{3,2,1,0:T(8,128)(2,1)}, bf16[3,2,256,256]{3,2,1,0:T(8,128)(2,1)}, bf16[3,2,256,256]{3,2,1,0:T(8,128)(2,1)}, bf16[3,2,256,256]{3,2,1,0:T(8,128)(2,1)}) custom-call(s32[2]{0:T(128)} %pad_add_fusion.place, f32[4,8,256,256]{3,2,1,0:T(8,128)} %bitcast.15, bf16[4,8,256,256]{3,2,1,0:T(8,128)(2,1)} %bitcast.23), custom_call_target="tpu_custom_call" | custom-call | flops 157286400 | bytes 7864320 | tf_op jit(solution)/shard_map/pallas_call | solution.py:310
  134.0 1.3 collective-permute-start.31
  135.3 1.3 collective-permute-start.25
  136.6 1.3 collective-permute-start.26
  137.9 1.6 collective-permute-start.24
  140.3 1.3 collective-permute-start.21
  141.6 13.9 %collective-permute-done.31.refs_9_ = bf16[3,2,256,256]{3,2,1,0:T(8,128)(2,1)} collective-permute-done((bf16[3,2,256,256]{3,2,1,0:T(8,128)(2,1)}, bf16[3,2,256,256]{3,2,1,0:T(8,128)(2,1)}, u32[]{:S(2)}, u32[]{:S(2)}) %collective-permute-start.31) | collective-permute-done | bytes 786464 | tf_op jit(solution)/shard_map/ppermute | solution.py:742
  156.7 5.2 %collective-permute-done.25.refs_0_ = bf16[3,2,256,256]{3,2,1,0:T(8,128)(2,1)} collective-permute-done((bf16[3,2,256,256]{3,2,1,0:T(8,128)(2,1)}, bf16[3,2,256,256]{3,2,1,0:T(8,128)(2,1)}, u32[]{:S(2)}, u32[]{:S(2)}) %collective-permute-start.25) | collective-permute-done | bytes 786464 | tf_op jit(solution)/shard_map/ppermute | solution.py:742
  161.9 1.3 collective-permute-start.32
  163.2 1.4 collective-permute-done.26.refs_1_
  164.6 4.7 %collective-permute-start.27 = (bf16[3,2,256,256]{3,2,1,0:T(8,128)(2,1)}, bf16[3,2,256,256]{3,2,1,0:T(8,128)(2,1)}, u32[]{:S(2)}, u32[]{:S(2)}) collective-permute-start(bf16[3,2,256,256]{3,2,1,0:T(8,128)(2,1)} %get-tuple-element.61), channel_id=1, source_target_pairs={{4,20},{14,30},{20,4},{30,14}} | collective-permute-start | bytes 2359304 | tf_op jit(solution)/shard_map/ppermute | solution.py:742
  169.2 1.3 collective-permute-start.34
  170.6 1.3 collective-permute-start.28
  171.9 1.3 collective-permute-start.29
  173.2 1.3 collective-permute-start.30
  174.5 5.5 %collective-permute-done.34.refs_11_ = bf16[3,256,256]{2,1,0:T(8,128)(2,1)} collective-permute-done((bf16[3,256,256]{2,1,0:T(8,128)(2,1)}, bf16[3,256,256]{2,1,0:T(8,128)(2,1)}, u32[]{:S(2)}, u32[]{:S(2)}) %collective-permute-start.34) | collective-permute-done | bytes 393248 | tf_op jit(solution)/shard_map/ppermute | solution.py:742
  182.3 30.1 %collective-permute-done.27.refs_2_ = bf16[3,2,256,256]{3,2,1,0:T(8,128)(2,1)} collective-permute-done((bf16[3,2,256,256]{3,2,1,0:T(8,128)(2,1)}, bf16[3,2,256,256]{3,2,1,0:T(8,128)(2,1)}, u32[]{:S(2)}, u32[]{:S(2)}) %collective-permute-start.27) | collective-permute-done | bytes 786464 | tf_op jit(solution)/shard_map/ppermute | solution.py:742
  213.6 3.6 %collective-permute-done.28.refs_3_ = bf16[3,2,256,256]{3,2,1,0:T(8,128)(2,1)} collective-permute-done((bf16[3,2,256,256]{3,2,1,0:T(8,128)(2,1)}, bf16[3,2,256,256]{3,2,1,0:T(8,128)(2,1)}, u32[]{:S(2)}, u32[]{:S(2)}) %collective-permute-start.28) | collective-permute-done | bytes 786464 | tf_op jit(solution)/shard_map/ppermute | solution.py:742
  217.2 1.3 collective-permute-start.35
  218.5 8.1 %sum_late.1 = (f32[3,256,256]{2,1,0:T(8,128)}, bf16[3,3,256,256]{3,2,1,0:T(8,128)(2,1)}, bf16[3,3,256,256]{3,2,1,0:T(8,128)(2,1)}, bf16[3,12,256,256]{3,2,1,0:T(8,128)(2,1)}) custom-call(s32[2]{0:T(128)} %pad_add_fusion.place, bf16[3,2,256,256]{3,2,1,0:T(8,128)(2,1)} %get-tuple-element.40.refs_0_, bf16[3,2,256,256]{3,2,1,0:T(8,128)(2,1)} %get-tuple-element.41.refs_1_, ...), custom_call_target="tpu_custom_call" | custom-call | flops 1811939328 | bytes 15728640 | tf_op jit(solution)/shard_map/sum_late/pallas_call | solution.py:469
  226.7 7.0 %rest_late.1 = (f32[3,256,256]{2,1,0:T(8,128)}, bf16[3,3,256,256]{3,2,1,0:T(8,128)(2,1)}) custom-call(s32[2]{0:T(128)} %pad_add_fusion.place, bf16[3,2,256,256]{3,2,1,0:T(8,128)(2,1)} %collective-permute-done.25.refs_0_, bf16[3,2,256,256]{3,2,1,0:T(8,128)(2,1)} %collective-permute-done.26.refs_1_, ...), custom_call_target="tpu_custom_call", output_to_operand_aliasing={{0}: (7, {}), {1}: (8, {})} | custom-call | flops 402653184 | bytes 4718592 | tf_op jit(solution)/shard_map/rest_late/pallas_call | solution.py:535
  233.7 6.4 %shard_map.52 = (f32[4,8,256,256]{3,2,1,0:T(8,128)}, bf16[3,256,256]{2,1,0:T(8,128)(2,1)}) custom-call(s32[2]{0:T(128)} %pad_add_fusion.place, f32[4,8,256,256]{3,2,1,0:T(8,128)} %get-tuple-element.58.out_in, bf16[3,256,256]{2,1,0:T(8,128)(2,1)} %get-tuple-element.59.refs_0_, ...), custom_call_target="tpu_custom_call", output_to_operand_aliasing={{0}: (1, {}), {1}: (2, {})} | custom-call | flops 1207959552 | bytes 7864320 | tf_op jit(solution)/shard_map/pallas_call | solution.py:685
  (46 shorter events, 15.1 us)
Async XLA Ops:
  4.2 10.9 %collective-permute-start.13 = (bf16[3,256,256]{2,1,0:T(8,128)(2,1)}, bf16[3,256,256]{2,1,0:T(8,128)(2,1)}, u32[]{:S(2)}, u32[]{:S(2)}) collective-permute-start(bf16[3,256,256]{2,1,0:T(8,128)(2,1)} %get-tuple-element.45.refs_14_.refs_10_), channel_id=1, source_target_pairs={{1,2},{2,3},{6,7},{7,4},{8,9},{11,8},{12,13},{13,14},{17,18},{18,1... | collective-permute-start | bytes 1179656 | tf_op jit(solution)/shard_map/ppermute | solution.py:742
  5.5 16.2 %collective-permute-start.14 = (bf16[3,256,256]{2,1,0:T(8,128)(2,1)}, bf16[3,256,256]{2,1,0:T(8,128)(2,1)}, u32[]{:S(2)}, u32[]{:S(2)}) collective-permute-start(bf16[3,256,256]{2,1,0:T(8,128)(2,1)} %get-tuple-element.45.refs_14_.refs_10_), channel_id=1, source_target_pairs={{1,3},{6,4},{11,9},{12,14},{17,19},{22,20},{27,25},{28,30}} | collective-permute-start | bytes 1179656 | tf_op jit(solution)/shard_map/ppermute | solution.py:742
  6.8 30.0 %collective-permute-start.2 = (bf16[3,2,256,256]{3,2,1,0:T(8,128)(2,1)}, bf16[3,2,256,256]{3,2,1,0:T(8,128)(2,1)}, u32[]{:S(2)}, u32[]{:S(2)}) collective-permute-start(bf16[3,2,256,256]{3,2,1,0:T(8,128)(2,1)} %get-tuple-element.40.refs_0_), channel_id=1, source_target_pairs={{0,1},{1,0},{2,3},{3,2},{4,5},{5,4},{6,7},{7,6},{8,9},{9,8},{10,11... | collective-permute-start | bytes 2359304 | tf_op jit(solution)/shard_map/ppermute | solution.py:742
  8.3 30.2 %collective-permute-start.5 = (bf16[3,2,256,256]{3,2,1,0:T(8,128)(2,1)}, bf16[3,2,256,256]{3,2,1,0:T(8,128)(2,1)}, u32[]{:S(2)}, u32[]{:S(2)}) collective-permute-start(bf16[3,2,256,256]{3,2,1,0:T(8,128)(2,1)} %get-tuple-element.41.refs_1_), channel_id=1, source_target_pairs={{0,2},{1,3},{2,0},{3,1},{4,6},{5,7},{6,4},{7,5},{8,10},{9,11},{10,... | collective-permute-start | bytes 2359304 | tf_op jit(solution)/shard_map/ppermute | solution.py:742
  10.3 32.9 %collective-permute-start.3 = (bf16[3,2,256,256]{3,2,1,0:T(8,128)(2,1)}, bf16[3,2,256,256]{3,2,1,0:T(8,128)(2,1)}, u32[]{:S(2)}, u32[]{:S(2)}) collective-permute-start(bf16[3,2,256,256]{3,2,1,0:T(8,128)(2,1)} %get-tuple-element.41.refs_1_), channel_id=1, source_target_pairs={{0,1},{1,0},{2,3},{3,2},{4,5},{5,4},{6,7},{7,6},{8,9},{9,8},{10,11... | collective-permute-start | bytes 2359304 | tf_op jit(solution)/shard_map/ppermute | solution.py:742
  15.1 12.3 %collective-permute-start.15 = (bf16[3,256,256]{2,1,0:T(8,128)(2,1)}, bf16[3,256,256]{2,1,0:T(8,128)(2,1)}, u32[]{:S(2)}, u32[]{:S(2)}) collective-permute-start(bf16[3,256,256]{2,1,0:T(8,128)(2,1)} %get-tuple-element.45.refs_14_.refs_10_), channel_id=1, source_target_pairs={{1,29},{2,30},{6,2},{7,3},{8,4},{11,7},{12,8},{13,9},{17,13},{18,1... | collective-permute-start | bytes 1179656 | tf_op jit(solution)/shard_map/ppermute | solution.py:742
  21.6 10.9 %collective-permute-start.16 = (bf16[3,256,256]{2,1,0:T(8,128)(2,1)}, bf16[3,256,256]{2,1,0:T(8,128)(2,1)}, u32[]{:S(2)}, u32[]{:S(2)}) collective-permute-start(bf16[3,256,256]{2,1,0:T(8,128)(2,1)} %get-tuple-element.45.refs_14_.refs_10_), channel_id=1, source_target_pairs={{1,25},{6,30},{11,3},{12,4},{17,9},{22,14},{27,19},{28,20}} | collective-permute-start | bytes 1179656 | tf_op jit(solution)/shard_map/ppermute | solution.py:742
  27.4 24.7 %collective-permute-start.4 = (bf16[3,2,256,256]{3,2,1,0:T(8,128)(2,1)}, bf16[3,2,256,256]{3,2,1,0:T(8,128)(2,1)}, u32[]{:S(2)}, u32[]{:S(2)}) collective-permute-start(bf16[3,2,256,256]{3,2,1,0:T(8,128)(2,1)} %get-tuple-element.40.refs_0_), channel_id=1, source_target_pairs={{0,2},{1,3},{2,0},{3,1},{4,6},{5,7},{6,4},{7,5},{8,10},{9,11},{10,... | collective-permute-start | bytes 2359304 | tf_op jit(solution)/shard_map/ppermute | solution.py:742
  32.5 21.9 %collective-permute-start.9 = (bf16[3,2,256,256]{3,2,1,0:T(8,128)(2,1)}, bf16[3,2,256,256]{3,2,1,0:T(8,128)(2,1)}, u32[]{:S(2)}, u32[]{:S(2)}) collective-permute-start(bf16[3,2,256,256]{3,2,1,0:T(8,128)(2,1)} %get-tuple-element.43), channel_id=1, source_target_pairs={{0,24},{1,25},{2,26},{3,27},{4,28},{5,29},{6,30},{7,31},{8,0},{9,1... | collective-permute-start | bytes 2359304 | tf_op jit(solution)/shard_map/ppermute | solution.py:742
  36.7 35.1 %collective-permute-start.11 = (bf16[3,2,256,256]{3,2,1,0:T(8,128)(2,1)}, bf16[3,2,256,256]{3,2,1,0:T(8,128)(2,1)}, u32[]{:S(2)}, u32[]{:S(2)}) collective-permute-start(bf16[3,2,256,256]{3,2,1,0:T(8,128)(2,1)} %get-tuple-element.44), channel_id=1, source_target_pairs={{0,8},{1,9},{2,10},{3,11},{4,12},{5,13},{6,14},{7,15},{8,16},{9,17... | collective-permute-start | bytes 2359304 | tf_op jit(solution)/shard_map/ppermute | solution.py:742
  38.5 33.7 %collective-permute-start.8 = (bf16[3,2,256,256]{3,2,1,0:T(8,128)(2,1)}, bf16[3,2,256,256]{3,2,1,0:T(8,128)(2,1)}, u32[]{:S(2)}, u32[]{:S(2)}) collective-permute-start(bf16[3,2,256,256]{3,2,1,0:T(8,128)(2,1)} %get-tuple-element.42.refs_8_), channel_id=1, source_target_pairs={{0,4},{1,5},{2,6},{3,7},{4,0},{5,1},{6,2},{7,3},{8,12},{9,13},{10,... | collective-permute-start | bytes 2359304 | tf_op jit(solution)/shard_map/ppermute | solution.py:742
  43.3 62.2 %collective-permute-start = (bf16[3,2,256,256]{3,2,1,0:T(8,128)(2,1)}, bf16[3,2,256,256]{3,2,1,0:T(8,128)(2,1)}, u32[]{:S(2)}, u32[]{:S(2)}) collective-permute-start(bf16[3,2,256,256]{3,2,1,0:T(8,128)(2,1)} %get-tuple-element.39), channel_id=1, source_target_pairs={{0,16},{1,17},{2,18},{3,19},{4,20},{5,21},{6,22},{7,23},{8,24},{9,... | collective-permute-start | bytes 2359304 | tf_op jit(solution)/shard_map/ppermute | solution.py:742
  52.1 59.8 %collective-permute-start.6 = (bf16[3,2,256,256]{3,2,1,0:T(8,128)(2,1)}, bf16[3,2,256,256]{3,2,1,0:T(8,128)(2,1)}, u32[]{:S(2)}, u32[]{:S(2)}) collective-permute-start(bf16[3,2,256,256]{3,2,1,0:T(8,128)(2,1)} %collective-permute-done.2.refs_2_), channel_id=1, source_target_pairs={{0,2},{1,3},{2,0},{3,1},{4,6},{5,7},{6,4},{7,5},{8,10},{9,11},{10,... | collective-permute-start | bytes 2359304 | tf_op jit(solution)/shard_map/ppermute | solution.py:742
  54.4 66.3 %collective-permute-start.7 = (bf16[3,2,256,256]{3,2,1,0:T(8,128)(2,1)}, bf16[3,2,256,256]{3,2,1,0:T(8,128)(2,1)}, u32[]{:S(2)}, u32[]{:S(2)}) collective-permute-start(bf16[3,2,256,256]{3,2,1,0:T(8,128)(2,1)} %collective-permute-done.5.refs_5_), channel_id=1, source_target_pairs={{0,1},{1,0},{2,3},{3,2},{4,5},{5,4},{6,7},{7,6},{8,9},{9,8},{10,11... | collective-permute-start | bytes 2359304 | tf_op jit(solution)/shard_map/ppermute | solution.py:742
  71.8 48.9 %collective-permute-start.10 = (bf16[3,2,256,256]{3,2,1,0:T(8,128)(2,1)}, bf16[3,2,256,256]{3,2,1,0:T(8,128)(2,1)}, u32[]{:S(2)}, u32[]{:S(2)}) collective-permute-start(bf16[3,2,256,256]{3,2,1,0:T(8,128)(2,1)} %collective-permute-done.9.refs_10_), channel_id=1, source_target_pairs={{0,4},{1,5},{2,6},{3,7},{4,0},{5,1},{6,2},{7,3},{8,12},{9,13},{10,... | collective-permute-start | bytes 2359304 | tf_op jit(solution)/shard_map/ppermute | solution.py:742
  72.2 48.5 %collective-permute-start.12 = (bf16[3,2,256,256]{3,2,1,0:T(8,128)(2,1)}, bf16[3,2,256,256]{3,2,1,0:T(8,128)(2,1)}, u32[]{:S(2)}, u32[]{:S(2)}) collective-permute-start(bf16[3,2,256,256]{3,2,1,0:T(8,128)(2,1)} %collective-permute-done.11.refs_12_), channel_id=1, source_target_pairs={{0,4},{1,5},{2,6},{3,7},{4,0},{5,1},{6,2},{7,3},{8,12},{9,13},{10,... | collective-permute-start | bytes 2359304 | tf_op jit(solution)/shard_map/ppermute | solution.py:742
  105.5 16.3 %collective-permute-start.1 = (bf16[3,2,256,256]{3,2,1,0:T(8,128)(2,1)}, bf16[3,2,256,256]{3,2,1,0:T(8,128)(2,1)}, u32[]{:S(2)}, u32[]{:S(2)}) collective-permute-start(bf16[3,2,256,256]{3,2,1,0:T(8,128)(2,1)} %collective-permute-done.refs_0_), channel_id=1, source_target_pairs={{0,4},{1,5},{2,6},{3,7},{4,0},{5,1},{6,2},{7,3},{8,12},{9,13},{10,... | collective-permute-start | bytes 2359304 | tf_op jit(solution)/shard_map/ppermute | solution.py:742
  112.0 22.0 %collective-permute-start.19 = (bf16[3,2,256,256]{3,2,1,0:T(8,128)(2,1)}, bf16[3,2,256,256]{3,2,1,0:T(8,128)(2,1)}, u32[]{:S(2)}, u32[]{:S(2)}) collective-permute-start(bf16[3,2,256,256]{3,2,1,0:T(8,128)(2,1)} %slice.11.refs_3_), channel_id=1, source_target_pairs={{0,28},{5,1},{10,6},{15,11},{16,12},{21,17},{26,22},{31,27}} | collective-permute-start | bytes 2359304 | tf_op jit(solution)/shard_map/ppermute | solution.py:742
  123.2 12.1 %collective-permute-start.17 = (bf16[3,256,256]{2,1,0:T(8,128)(2,1)}, bf16[3,256,256]{2,1,0:T(8,128)(2,1)}, u32[]{:S(2)}, u32[]{:S(2)}) collective-permute-start(bf16[3,256,256]{2,1,0:T(8,128)(2,1)} %get-tuple-element.55.refs_0_), channel_id=1, source_target_pairs={{0,1},{5,6},{10,11},{15,12},{16,17},{21,22},{26,27},{31,28}} | collective-permute-start | bytes 1179656 | tf_op jit(solution)/shard_map/ppermute | solution.py:742
  124.7 12.0 %collective-permute-start.18 = (bf16[3,256,256]{2,1,0:T(8,128)(2,1)}, bf16[3,256,256]{2,1,0:T(8,128)(2,1)}, u32[]{:S(2)}, u32[]{:S(2)}) collective-permute-start(bf16[3,256,256]{2,1,0:T(8,128)(2,1)} %get-tuple-element.55.refs_0_), channel_id=1, source_target_pairs={{0,28},{5,1},{10,6},{15,11},{16,12},{21,17},{26,22},{31,27}} | collective-permute-start | bytes 1179656 | tf_op jit(solution)/shard_map/ppermute | solution.py:742
  126.1 11.8 %collective-permute-start.20 = (bf16[3,256,256]{2,1,0:T(8,128)(2,1)}, bf16[3,256,256]{2,1,0:T(8,128)(2,1)}, u32[]{:S(2)}, u32[]{:S(2)}) collective-permute-start(bf16[3,256,256]{2,1,0:T(8,128)(2,1)} %get-tuple-element.55.refs_0_), channel_id=1, source_target_pairs={{0,2},{5,7},{10,8},{15,13},{16,18},{21,23},{26,24},{31,29}} | collective-permute-start | bytes 1179656 | tf_op jit(solution)/shard_map/ppermute | solution.py:742
  127.6 11.9 %collective-permute-start.22 = (bf16[3,256,256]{2,1,0:T(8,128)(2,1)}, bf16[3,256,256]{2,1,0:T(8,128)(2,1)}, u32[]{:S(2)}, u32[]{:S(2)}) collective-permute-start(bf16[3,256,256]{2,1,0:T(8,128)(2,1)} %get-tuple-element.55.refs_0_), channel_id=1, source_target_pairs={{0,24},{5,29},{10,2},{15,7},{16,8},{21,13},{26,18},{31,23}} | collective-permute-start | bytes 1179656 | tf_op jit(solution)/shard_map/ppermute | solution.py:742
  134.0 21.4 %collective-permute-start.31 = (bf16[3,2,256,256]{3,2,1,0:T(8,128)(2,1)}, bf16[3,2,256,256]{3,2,1,0:T(8,128)(2,1)}, u32[]{:S(2)}, u32[]{:S(2)}) collective-permute-start(bf16[3,2,256,256]{3,2,1,0:T(8,128)(2,1)} %get-tuple-element.63.refs_8_), channel_id=1, source_target_pairs={{0,4},{10,14},{16,20},{26,30}} | collective-permute-start | bytes 2359304 | tf_op jit(solution)/shard_map/ppermute | solution.py:742
  135.3 26.6 %collective-permute-start.25 = (bf16[3,2,256,256]{3,2,1,0:T(8,128)(2,1)}, bf16[3,2,256,256]{3,2,1,0:T(8,128)(2,1)}, u32[]{:S(2)}, u32[]{:S(2)}) collective-permute-start(bf16[3,2,256,256]{3,2,1,0:T(8,128)(2,1)} %get-tuple-element.60), channel_id=1, source_target_pairs={{6,14},{12,4},{22,30},{28,20}} | collective-permute-start | bytes 2359304 | tf_op jit(solution)/shard_map/ppermute | solution.py:742
  136.6 27.9 %collective-permute-start.26 = (bf16[3,2,256,256]{3,2,1,0:T(8,128)(2,1)}, bf16[3,2,256,256]{3,2,1,0:T(8,128)(2,1)}, u32[]{:S(2)}, u32[]{:S(2)}) collective-permute-start(bf16[3,2,256,256]{3,2,1,0:T(8,128)(2,1)} %get-tuple-element.60), channel_id=1, source_target_pairs={{2,14},{8,4},{18,30},{24,20}} | collective-permute-start | bytes 2359304 | tf_op jit(solution)/shard_map/ppermute | solution.py:742
  137.9 31.3 %collective-permute-start.24 = (bf16[3,2,256,256]{3,2,1,0:T(8,128)(2,1)}, bf16[3,2,256,256]{3,2,1,0:T(8,128)(2,1)}, u32[]{:S(2)}, u32[]{:S(2)}) collective-permute-start(bf16[3,2,256,256]{3,2,1,0:T(8,128)(2,1)} %collective-permute-done.19.refs_6_), channel_id=1, source_target_pairs={{1,29},{6,2},{11,7},{12,8},{17,13},{22,18},{27,23},{28,24}} | collective-permute-start | bytes 2359304 | tf_op jit(solution)/shard_map/ppermute | solution.py:742
  140.3 30.3 %collective-permute-start.21 = (bf16[3,256,256]{2,1,0:T(8,128)(2,1)}, bf16[3,256,256]{2,1,0:T(8,128)(2,1)}, u32[]{:S(2)}, u32[]{:S(2)}) collective-permute-start(bf16[3,256,256]{2,1,0:T(8,128)(2,1)} %get-tuple-element.57.refs_0_), channel_id=1, source_target_pairs={{0,3},{1,2},{5,4},{6,7},{10,9},{11,8},{12,13},{15,14},{16,19},{17,... | collective-permute-start | bytes 1179656 | tf_op jit(solution)/shard_map/ppermute | solution.py:742
  155.5 16.4 %collective-permute-start.23 = (bf16[3,256,256]{2,1,0:T(8,128)(2,1)}, bf16[3,256,256]{2,1,0:T(8,128)(2,1)}, u32[]{:S(2)}, u32[]{:S(2)}) collective-permute-start(bf16[3,256,256]{2,1,0:T(8,128)(2,1)} %get-tuple-element.57.refs_0_), channel_id=1, source_target_pairs={{0,20},{1,29},{5,25},{6,2},{10,30},{11,7},{12,8},{15,3},{16,4},{17... | collective-permute-start | bytes 1179656 | tf_op jit(solution)/shard_map/ppermute | solution.py:742
  161.9 11.2 %collective-permute-start.32 = (bf16[3,256,256]{2,1,0:T(8,128)(2,1)}, bf16[3,256,256]{2,1,0:T(8,128)(2,1)}, u32[]{:S(2)}, u32[]{:S(2)}) collective-permute-start(bf16[3,256,256]{2,1,0:T(8,128)(2,1)} %get-tuple-element.57.refs_0_), channel_id=1, source_target_pairs={{1,3},{6,4},{11,9},{12,14},{17,19},{22,20},{27,25},{28,30}} | collective-permute-start | bytes 1179656 | tf_op jit(solution)/shard_map/ppermute | solution.py:742
  164.6 47.8 %collective-permute-start.27 = (bf16[3,2,256,256]{3,2,1,0:T(8,128)(2,1)}, bf16[3,2,256,256]{3,2,1,0:T(8,128)(2,1)}, u32[]{:S(2)}, u32[]{:S(2)}) collective-permute-start(bf16[3,2,256,256]{3,2,1,0:T(8,128)(2,1)} %get-tuple-element.61), channel_id=1, source_target_pairs={{4,20},{14,30},{20,4},{30,14}} | collective-permute-start | bytes 2359304 | tf_op jit(solution)/shard_map/ppermute | solution.py:742
  169.2 10.7 %collective-permute-start.34 = (bf16[3,256,256]{2,1,0:T(8,128)(2,1)}, bf16[3,256,256]{2,1,0:T(8,128)(2,1)}, u32[]{:S(2)}, u32[]{:S(2)}) collective-permute-start(bf16[3,256,256]{2,1,0:T(8,128)(2,1)} %get-tuple-element.57.refs_0_), channel_id=1, source_target_pairs={{1,25},{6,30},{11,3},{12,4},{17,9},{22,14},{27,19},{28,20}} | collective-permute-start | bytes 1179656 | tf_op jit(solution)/shard_map/ppermute | solution.py:742
  170.6 46.7 %collective-permute-start.28 = (bf16[3,2,256,256]{3,2,1,0:T(8,128)(2,1)}, bf16[3,2,256,256]{3,2,1,0:T(8,128)(2,1)}, u32[]{:S(2)}, u32[]{:S(2)}) collective-permute-start(bf16[3,2,256,256]{3,2,1,0:T(8,128)(2,1)} %get-tuple-element.61), channel_id=1, source_target_pairs={{0,20},{10,30},{16,4},{26,14}} | collective-permute-start | bytes 2359304 | tf_op jit(solution)/shard_map/ppermute | solution.py:742
  171.9 54.8 %collective-permute-start.29 = (bf16[3,2,256,256]{3,2,1,0:T(8,128)(2,1)}, bf16[3,2,256,256]{3,2,1,0:T(8,128)(2,1)}, u32[]{:S(2)}, u32[]{:S(2)}) collective-permute-start(bf16[3,2,256,256]{3,2,1,0:T(8,128)(2,1)} %get-tuple-element.62), channel_id=1, source_target_pairs={{6,30},{12,20},{22,14},{28,4}} | collective-permute-start | bytes 2359304 | tf_op jit(solution)/shard_map/ppermute | solution.py:742
  173.2 53.5 %collective-permute-start.30 = (bf16[3,2,256,256]{3,2,1,0:T(8,128)(2,1)}, bf16[3,2,256,256]{3,2,1,0:T(8,128)(2,1)}, u32[]{:S(2)}, u32[]{:S(2)}) collective-permute-start(bf16[3,2,256,256]{3,2,1,0:T(8,128)(2,1)} %get-tuple-element.62), channel_id=1, source_target_pairs={{2,30},{8,20},{18,14},{24,4}} | collective-permute-start | bytes 2359304 | tf_op jit(solution)/shard_map/ppermute | solution.py:742
  180.0 53.7 %collective-permute-start.36 = (bf16[3,2,256,256]{3,2,1,0:T(8,128)(2,1)}, bf16[3,2,256,256]{3,2,1,0:T(8,128)(2,1)}, u32[]{:S(2)}, u32[]{:S(2)}) collective-permute-start(bf16[3,2,256,256]{3,2,1,0:T(8,128)(2,1)} %collective-permute-done.24.refs_8_), channel_id=1, source_target_pairs={{2,30},{7,3},{8,4},{13,9},{18,14},{23,19},{24,20},{29,25}} | collective-permute-start | bytes 2359304 | tf_op jit(solution)/shard_map/ppermute | solution.py:742
  212.3 21.3 %collective-permute-start.33 = (bf16[3,256,256]{2,1,0:T(8,128)(2,1)}, bf16[3,256,256]{2,1,0:T(8,128)(2,1)}, u32[]{:S(2)}, u32[]{:S(2)}) collective-permute-start(bf16[3,256,256]{2,1,0:T(8,128)(2,1)} %get-tuple-element.59.refs_0_), channel_id=1, source_target_pairs={{2,3},{7,4},{8,9},{13,14},{18,19},{23,20},{24,25},{29,30}} | collective-permute-start | bytes 1179656 | tf_op jit(solution)/shard_map/ppermute | solution.py:742
  217.2 16.4 %collective-permute-start.35 = (bf16[3,256,256]{2,1,0:T(8,128)(2,1)}, bf16[3,256,256]{2,1,0:T(8,128)(2,1)}, u32[]{:S(2)}, u32[]{:S(2)}) collective-permute-start(bf16[3,256,256]{2,1,0:T(8,128)(2,1)} %get-tuple-element.59.refs_0_), channel_id=1, source_target_pairs={{2,30},{7,3},{8,4},{13,9},{18,14},{23,19},{24,20},{29,25}} | collective-permute-start | bytes 1179656 | tf_op jit(solution)/shard_map/ppermute | solution.py:742
